TPU v7x, 128 devices: a whole 4x4x4 slice. The times are simulated.
128 devices in a mesh: row: 8 (over z, core), col: 16 (over x, y).
Axes of the slice: x: 4, y: 4, z: 4, core: 2. Of those that a mesh axis runs over, the one named last changes fastest.
Arguments:
- right_side: float32 [16, 2048, 6144], P(None, 'row', 'col'), may hold values from -100 to 100
- cond_x: float32 [2048, 6144], P('row', 'col'), may hold values from 0.25 to 4
- cond_y: float32 [2048, 6144], P('row', 'col'), may hold values from 0.25 to 4
- pad_mask: int32 [2048, 6144], P('row', 'col'), may hold values 0 or 1
Outputs:
- solution: float32 [16, 2048, 6144], P(None, 'row', 'col')
- residual: float32 [16, 2048, 6144], P(None, 'row', 'col')
All inputs are finite; a program needn't handle non-finite values. No bound on the sum of `pad_mask` on one device may be relied on, other than what follows from the above.
Results may differ from a plain program's by a relative error of at most 0.0003.
Values sent between devices are 32-bit elements; how exact they have to be, the bound alone decides.
A program may use at most 128 MiB of HBM per device.

v0:
```python
import jax
import jax.numpy as jnp
from jax import lax
from jax.sharding import Mesh
from jax.sharding import PartitionSpec as P

ITERS = 3
ROW = ("row_0", "row_1")
COL = ("col_0", "col_1")
ROW_COL = ("row_0", "row_1", "col_0", "col_1")


exact_precision = lax.Precision.HIGHEST


def passed_along(shard, axis, by):
    peers = lax.axis_size(axis)
    pairs = [(i, i + by) for i in range(peers) if 0 <= i + by < peers]
    return lax.ppermute(shard, axis, pairs)


def with_halo(shard, sides, width):
    edges = {}
    for axis, dim in sides:
        peers, length = (lax.axis_size(axis), shard.shape[dim])
        up = [(i, (i + 1) % peers) for i in range(peers - 1)]
        last = lax.slice_in_dim(shard, length - width, length, axis=dim)
        first = lax.slice_in_dim(shard, 0, width, axis=dim)
        edges[dim] = (
            lax.ppermute(last, axis, up),
            lax.ppermute(first, axis, [(b, a) for a, b in up]),
        )
    done = []
    for _, dim in sides:
        low, high = edges[dim]
        around = [(width, width) if d in done else (0, 0) for d in range(shard.ndim)]
        shard = jnp.concatenate([jnp.pad(low, around), shard, jnp.pad(high, around)], axis=dim)
        done.append(dim)
    return shard


def one_axis_at_a_time(shard, axes):
    for axis in axes:
        shard = lax.psum(shard, axis)
    return shard


def neighbour_sum(padded, cond_x, cond_above, cond_y, cond_left):
    total = cond_x * padded[:, 2:, 1:-1] + cond_above * padded[:, :-2, 1:-1]
    return total + cond_y * padded[:, 1:-1, 2:] + cond_left * padded[:, 1:-1, :-2]


def gram(left, right):
    return jnp.einsum("kab,lab->kl", left, right, precision=exact_precision)


def combine(field, matrix):
    return jnp.einsum("kab,kl->lab", field, matrix, precision=exact_precision)


def small_solve(matrix, right):
    factor = jnp.linalg.cholesky(matrix)
    return jax.scipy.linalg.cho_solve((factor, True), right)


def shards(right_side, cond_x, cond_y, pad_mask):
    pad_nodes = pad_mask.astype(jnp.float32)
    free_nodes = 1.0 - pad_nodes
    upper_row = passed_along(cond_x[-1:], ROW, 1)
    cond_above = jnp.concatenate([upper_row, cond_x[:-1]], 0)
    left_column = passed_along(cond_y[:, -1:], COL, 1)
    cond_left = jnp.concatenate([left_column, cond_y[:, :-1]], 1)
    diagonal = free_nodes * (cond_x + cond_above + cond_y + cond_left) + pad_nodes
    inverse = 1.0 / diagonal
    solution = jnp.zeros_like(right_side)
    residual = right_side
    precond = residual * inverse
    direction = precond
    gram_now = one_axis_at_a_time(gram(residual, precond), ROW_COL)
    for iteration in range(ITERS):
        padded = with_halo(free_nodes * direction, ((ROW, 1), (COL, 2)), 1)
        image = pad_nodes * direction + free_nodes * (
            diagonal * direction - neighbour_sum(padded, cond_x, cond_above, cond_y, cond_left)
        )
        weighted = image * inverse
        curvature, cross_term, image_term = (
            one_axis_at_a_time(gram(direction, image), ROW_COL),
            one_axis_at_a_time(gram(image, precond), ROW_COL),
            one_axis_at_a_time(gram(image, weighted), ROW_COL),
        )
        alpha_block = small_solve(curvature, gram_now)
        solution = solution + combine(direction, alpha_block)
        residual = residual - combine(image, alpha_block)
        precond = residual * inverse
        mixed = jnp.dot(alpha_block.T, cross_term, precision=exact_precision)
        quadratic = jnp.dot(
            jnp.dot(alpha_block.T, image_term, precision=exact_precision),
            alpha_block,
            precision=exact_precision,
        )
        gram_next = gram_now - mixed - mixed.T + quadratic
        beta_block = small_solve(gram_now, gram_next)
        direction = precond + combine(direction, beta_block)
        gram_now = gram_next
    return (solution, residual)


def solution(mesh):
    split = Mesh(mesh.devices.reshape(4, 2, 4, 4), ("row_0", "row_1", "col_0", "col_1"))
    in_specs = (P(None, ROW, COL), P(ROW, COL), P(ROW, COL), P(ROW, COL))
    out_specs = (P(None, ROW, COL), P(None, ROW, COL))
    return jax.shard_map(
        shards, mesh=split, in_specs=in_specs, out_specs=out_specs, check_vma=False
    )
```

profile of v0, /device:TPU:1, one launch (start us, length us, event | category | flops | bytes accessed | tf_op | source)
XLA Modules:
  0.0 505.5 jit_solution(17853337915778137059)
XLA Ops:
  1.5 5.2 %collective-permute-start = (f32[1,384]{1,0:T(1,128)S(1)}, f32[1,384]{1,0:T(1,128)S(1)}, u32[]{:S(2)}, u32[]{:S(2)}) collective-permute-start(f32[1,384]{1,0:T(1,128)S(1)} %slice.108), channel_id=1, source_target_pairs={{0,16},{16,32},{32,48},{48,64},{64,80},{80,96},{96,112},{1,17},{17... | collective-permute-start | bytes 4616 | tf_op jit(solution)/shard_map/ppermute | solution.py:19
  7.7 3.2 collective-permute-start.1
  10.9 1.8 convert_element_type.10
  13.0 2.8 multiply_add_fusion.2
  16.8 4.0 multiply_multiply_fusion
  20.9 2.7 copy-done.4
  23.6 2.0 fusion.126
  25.6 2.9 collective-permute-start.3
  28.5 1.9 collective-permute-start.2
  30.5 2.5 copy.30
  34.0 4.2 collective-permute-start.5
  38.3 1.7 collective-permute-start.4
  39.9 30.3 %fusion.84 = f32[16,16]{0,1:T(8,128)S(1)} fusion(f32[16,256,384]{2,1,0:T(8,128)} %param.7, f32[256,384]{1,0:T(8,128)S(1)} %fusion.89), kind=kOutput, calls=%fused_computation.114 | convolution fusion | flops 303562752 | bytes 6685696 | tf_op jit(solution)/shard_map/kab,lab->kl/dot_general | solution.py:54
  70.2 2.4 copy.31
  72.6 2.4 copy.33
  75.0 20.2 %fusion.14 = f32[16,256,384]{2,0,1:T(8,128)S(1)} fusion(f32[16,256,1]{2,0,1:T(8,128)} %copy.33, f32[16,1,384]{2,0,1:T(8,128)S(1)} %collective-permute-done.2, f32[16,256,384]{2,0,1:T(8,128)} %copy-done.4, f32[16,1,384]{2,0,1:T(8,128)S(1)} %collective-permute-done.3, f32[16,256,1]{2,0,1:T(8,128)} %copy.31, f32[16,256,384]{2,1,0:T(8,128)} %param.7, ...), kind=kLoop, calls=%fused_computation.17 | loop fusion | flops 42467328 | bytes 22102016 | tf_op jit(solution)/shard_map/add | solution.py:82
  95.3 8.1 %fusion.78 = f32[16,16]{1,0:T(8,128)S(1)} fusion(f32[16,256,384]{2,0,1:T(8,128)S(1)} %fusion.14, f32[256,384]{1,0:T(8,128)S(1)} %fusion.89), kind=kOutput, calls=%fused_computation.105 | convolution fusion | flops 303562752 | bytes 6685696 | tf_op jit(solution)/shard_map/kab,lab->kl/dot_general | solution.py:54
  103.4 10.6 %fusion.75 = f32[16,16]{1,0:T(8,128)S(1)} fusion(f32[16,256,384]{2,0,1:T(8,128)S(1)} %fusion.14, f32[16,256,384]{2,1,0:T(8,128)S(1)} %bitcast.144, f32[256,384]{1,0:T(8,128)S(1)} %fusion.89), kind=kOutput, calls=%fused_computation.104 | convolution fusion | flops 303562752 | bytes 12977152 | tf_op jit(solution)/shard_map/kab,lab->kl/dot_general | solution.py:54
  114.0 10.6 %fusion.72 = f32[16,16]{0,1:T(8,128)S(1)} fusion(f32[16,256,384]{2,0,1:T(8,128)S(1)} %fusion.14, f32[16,256,384]{2,1,0:T(8,128)S(1)} %bitcast.144, f32[256,384]{1,0:T(8,128)S(1)} %fusion.89), kind=kOutput, calls=%fused_computation.103 | convolution fusion | flops 303562752 | bytes 12977152 | tf_op jit(solution)/shard_map/kab,lab->kl/dot_general | solution.py:54
  124.6 13.1 %all-reduce.11 = (f32[16,16]{0,1:T(8,128)S(1)}, f32[16,16]{0,1:T(8,128)S(1)}, f32[16,16]{1,0:T(8,128)S(1)}, f32[16,16]{1,0:T(8,128)S(1)}) all-reduce(f32[16,16]{0,1:T(8,128)S(1)} %fusion.84, f32[16,16]{0,1:T(8,128)S(1)} %fusion.72, f32[16,16]{1,0:T(8,128)S(1)} %fusion.78, ...), channel_id=1, replica_groups=mesh['row_0'=4,'row_1'=2,'col_0'=4,'col_1'=4] {'row_0'}, use_global_device_ids=true, to_apply=%region_6.8 | all-reduce | flops 1024 | bytes 8192 | tf_op jit(solution)/shard_map/psum | solution.py:44
  137.7 9.1 %all-reduce.13 = (f32[16,16]{0,1:T(8,128)S(1)}, f32[16,16]{0,1:T(8,128)S(1)}, f32[16,16]{1,0:T(8,128)S(1)}, f32[16,16]{1,0:T(8,128)S(1)}) all-reduce(f32[16,16]{0,1:T(8,128)S(1)} %get-tuple-element.25, f32[16,16]{0,1:T(8,128)S(1)} %get-tuple-element.26, ...), channel_id=1, replica_groups=mesh['row_0'=4,'row_1'=2,'col_0'=4,'col_1'=4] {'row_1'}, use_global_device_ids=true, to_apply=%region_7.9 | all-reduce | flops 1024 | bytes 8192 | tf_op jit(solution)/shard_map/psum | solution.py:44
  146.8 18.6 %all-reduce.9 = (f32[16,16]{0,1:T(8,128)S(1)}, f32[16,16]{0,1:T(8,128)S(1)}, f32[16,16]{1,0:T(8,128)S(1)}, f32[16,16]{1,0:T(8,128)S(1)}) all-reduce(f32[16,16]{0,1:T(8,128)S(1)} %get-tuple-element.32, f32[16,16]{0,1:T(8,128)S(1)} %get-tuple-element.33, ...), channel_id=1, replica_groups=mesh['row_0'=4,'row_1'=2,'col_0'=4,'col_1'=4] {'col_0'}, use_global_device_ids=true, to_apply=%region_8.10 | all-reduce | flops 1024 | bytes 8192 | tf_op jit(solution)/shard_map/psum | solution.py:44
  165.4 11.0 %all-reduce.7 = (f32[16,16]{0,1:T(8,128)S(1)}, f32[16,16]{0,1:T(8,128)S(1)}, f32[16,16]{1,0:T(8,128)S(1)}, f32[16,16]{1,0:T(8,128)S(1)}) all-reduce(f32[16,16]{0,1:T(8,128)S(1)} %get-tuple-element.18, f32[16,16]{0,1:T(8,128)S(1)} %get-tuple-element.19, ...), channel_id=1, replica_groups=mesh['row_0'=4,'row_1'=2,'col_0'=4,'col_1'=4] {'col_1'}, use_global_device_ids=true, to_apply=%region_9.11 | all-reduce | flops 1024 | bytes 8192 | tf_op jit(solution)/shard_map/psum | solution.py:44
  184.9 13.2 %copy_subtract_fusion = f32[16,256,384]{2,0,1:T(8,128)} fusion(f32[16,256,384]{2,1,0:T(8,128)} %param.7, f32[16,256,384]{2,0,1:T(8,128)} %copy-done.1, f32[16,16]{1,0:T(8,128)S(1)} %fusion.117), kind=kOutput, calls=%fused_computation.88 | convolution fusion | flops 303562752 | bytes 18875392 | tf_op jit(solution)/shard_map/kab,kl->lab/dot_general | solution.py:58
  199.3 15.0 %broadcast_multiply_fusion.1 = (f32[16,256,384]{2,0,1:T(8,128)S(1)}, f32[16,256,384]{2,0,1:T(8,128)}) fusion(f32[256,384]{1,0:T(8,128)S(1)} %get-tuple-element.52, f32[16,16,1]{0,1,2:T(8,128)S(1)} %convolution_bitcast_fusion.4, f32[16,256,384]{2,1,0:T(8,128)} %param.7, f32[256,384]{1,0:T(8,128)S(1)} %fusion.89, f32[16,256,384]{2,0,1:T(8,128)} %copy_subtract_fusion), kind=kOutput, calls=%fused_computation.91 | convolution fusion | flops 308281344 | bytes 25953280 | tf_op jit(solution)/shard_map/kab,kl->lab/dot_general | solution.py:58
  214.4 2.6 copy-done.5
  217.0 2.0 fusion.124
  221.1 7.4 %collective-permute-start.7 = (f32[16,1,384]{2,0,1:T(8,128)S(1)}, f32[16,1,384]{2,0,1:T(8,128)S(1)}, u32[]{:S(2)}, u32[]{:S(2)}) collective-permute-start(f32[16,1,384]{2,0,1:T(8,128)S(1)} %get-tuple-element.46), channel_id=1, source_target_pairs={{0,16},{16,32},{32,48},{48,64},{64,80},{80,96},{96,112},{1,17},{17... | collective-permute-start | bytes 73736 | tf_op jit(solution)/shard_map/ppermute | solution.py:30
  228.6 3.1 collective-permute-start.6
  231.7 2.5 copy.43
  235.3 2.3 collective-permute-start.9
  240.7 1.7 collective-permute-done.8
  242.4 2.4 copy.44
  244.9 2.4 copy.46
  247.3 18.5 %fusion.34 = f32[16,256,384]{2,0,1:T(8,128)S(1)} fusion(f32[16,256,1]{2,0,1:T(8,128)} %copy.46, f32[16,1,384]{2,0,1:T(8,128)S(1)} %collective-permute-done.6, f32[16,256,384]{2,0,1:T(8,128)} %copy-done.5, f32[16,1,384]{2,0,1:T(8,128)S(1)} %collective-permute-done.7, f32[16,256,1]{2,0,1:T(8,128)} %copy.44, f32[16,256,384]{2,0,1:T(8,128)} %get-tuple-element.54, ...), kind=kLoop, calls=%fused_computation.46 | loop fusion | flops 40894464 | bytes 21708800 | tf_op jit(solution)/shard_map/add | solution.py:82
  265.8 8.1 %fusion.81 = f32[16,16]{1,0:T(8,128)S(1)} fusion(f32[16,256,384]{2,0,1:T(8,128)S(1)} %fusion.34, f32[256,384]{1,0:T(8,128)S(1)} %fusion.89), kind=kOutput, calls=%fused_computation.106 | convolution fusion | flops 303562752 | bytes 6685696 | tf_op jit(solution)/shard_map/kab,lab->kl/dot_general | solution.py:54
  273.9 8.1 %fusion.69 = f32[16,16]{1,0:T(8,128)S(1)} fusion(f32[16,256,384]{2,0,1:T(8,128)S(1)} %fusion.34, f32[16,256,384]{2,0,1:T(8,128)S(1)} %bitcast.150, f32[256,384]{1,0:T(8,128)S(1)} %fusion.89), kind=kOutput, calls=%fused_computation.102 | convolution fusion | flops 303562752 | bytes 12977152 | tf_op jit(solution)/shard_map/kab,lab->kl/dot_general | solution.py:54
  282.1 8.4 %convolution_bitcast_fusion.3 = f32[16,16]{0,1:T(8,128)S(1)} fusion(f32[16,256,384]{2,0,1:T(8,128)S(1)} %bitcast.148, f32[16,256,384]{2,0,1:T(8,128)S(1)} %fusion.34), kind=kOutput, calls=%fused_computation.111 | convolution fusion | flops 301989888 | bytes 12583936 | tf_op jit(solution)/shard_map/kab,lab->kl/dot_general | solution.py:54
  290.5 12.3 %all-reduce.10 = (f32[16,16]{0,1:T(8,128)S(1)}, f32[16,16]{1,0:T(8,128)S(1)}, f32[16,16]{1,0:T(8,128)S(1)}) all-reduce(f32[16,16]{0,1:T(8,128)S(1)} %convolution_bitcast_fusion.3, f32[16,16]{1,0:T(8,128)S(1)} %fusion.81, f32[16,16]{1,0:T(8,128)S(1)} %fusion.69), channel_id=1, replica_groups=mesh['row_0'=4,'row_1'=2,'col_0'=4,'col_1'=4] {'row_0'}, use_global_device_ids=true, to_apply=%region_18.21 | all-reduce | flops 768 | bytes 6144 | tf_op jit(solution)/shard_map/psum | solution.py:44
  302.7 8.5 %all-reduce.12 = (f32[16,16]{0,1:T(8,128)S(1)}, f32[16,16]{1,0:T(8,128)S(1)}, f32[16,16]{1,0:T(8,128)S(1)}) all-reduce(f32[16,16]{0,1:T(8,128)S(1)} %get-tuple-element.22, f32[16,16]{1,0:T(8,128)S(1)} %get-tuple-element.23, f32[16,16]{1,0:T(8,128)S(1)} %get-tuple-element.24), channel_id=1, replica_groups=mesh['row_0'=4,'row_1'=2,'col_0'=4,'col_1'=4] {'row_1'}, use_global_device_ids=true, to_apply=%region_19.22 | all-reduce | flops 768 | bytes 6144 | tf_op jit(solution)/shard_map/psum | solution.py:44
  311.2 11.8 %all-reduce.8 = (f32[16,16]{0,1:T(8,128)S(1)}, f32[16,16]{1,0:T(8,128)S(1)}, f32[16,16]{1,0:T(8,128)S(1)}) all-reduce(f32[16,16]{0,1:T(8,128)S(1)} %get-tuple-element.29, f32[16,16]{1,0:T(8,128)S(1)} %get-tuple-element.30, f32[16,16]{1,0:T(8,128)S(1)} %get-tuple-element.31), channel_id=1, replica_groups=mesh['row_0'=4,'row_1'=2,'col_0'=4,'col_1'=4] {'col_0'}, use_global_device_ids=true, to_apply=%region_20.23 | all-reduce | flops 768 | bytes 6144 | tf_op jit(solution)/shard_map/psum | solution.py:44
  323.0 14.8 %all-reduce.6 = (f32[16,16]{0,1:T(8,128)S(1)}, f32[16,16]{1,0:T(8,128)S(1)}, f32[16,16]{1,0:T(8,128)S(1)}) all-reduce(f32[16,16]{0,1:T(8,128)S(1)} %get-tuple-element.15, f32[16,16]{1,0:T(8,128)S(1)} %get-tuple-element.16, f32[16,16]{1,0:T(8,128)S(1)} %get-tuple-element.17), channel_id=1, replica_groups=mesh['row_0'=4,'row_1'=2,'col_0'=4,'col_1'=4] {'col_1'}, use_global_device_ids=true, to_apply=%region_21.24 | all-reduce | flops 768 | bytes 6144 | tf_op jit(solution)/shard_map/psum | solution.py:44
  342.1 10.7 %convolution_subtract_fusion.1 = f32[16,256,384]{2,0,1:T(8,128)} fusion(f32[16,256,384]{2,0,1:T(8,128)} %copy_subtract_fusion, f32[16,256,384]{2,0,1:T(8,128)} %copy-done.2, f32[16,16]{1,0:T(8,128)S(1)} %fusion.106), kind=kOutput, calls=%fused_computation.101 | convolution fusion | flops 303562752 | bytes 18875392 | tf_op jit(solution)/shard_map/kab,kl->lab/dot_general | solution.py:58
  353.9 11.0 %broadcast_multiply_fusion = (f32[16,256,384]{2,0,1:T(8,128)S(1)}, f32[16,256,384]{2,0,1:T(8,128)}) fusion(f32[256,384]{1,0:T(8,128)S(1)} %get-tuple-element.52, f32[16,16,1]{0,1,2:T(8,128)S(1)} %convolution_bitcast_fusion.2, f32[16,256,384]{2,0,1:T(8,128)} %get-tuple-element.54, f32[16,256,384]{2,0,1:T(8,128)} %convolution_subtract_fusion.1, ...), kind=kOutput, calls=%fused_computation.90 | convolution fusion | flops 306708480 | bytes 25953280 | tf_op jit(solution)/shard_map/kab,kl->lab/dot_general | solution.py:58
  364.9 2.6 copy-done.6
  367.5 2.0 fusion.122
  369.6 8.9 %collective-permute-start.11 = (f32[16,1,384]{2,0,1:T(8,128)S(1)}, f32[16,1,384]{2,0,1:T(8,128)S(1)}, u32[]{:S(2)}, u32[]{:S(2)}) collective-permute-start(f32[16,1,384]{2,0,1:T(8,128)S(1)} %get-tuple-element.42), channel_id=1, source_target_pairs={{0,16},{16,32},{32,48},{48,64},{64,80},{80,96},{96,112},{1,17},{17... | collective-permute-start | bytes 73736 | tf_op jit(solution)/shard_map/ppermute | solution.py:30
  378.5 2.0 collective-permute-start.10
  380.4 2.5 copy.54
  386.8 9.4 %fusion.104 = f32[16,256,384]{2,0,1:T(8,128)} fusion(f32[16,256,384]{2,0,1:T(8,128)} %get-tuple-element.54, f32[16,16]{1,0:T(8,128)S(1)} %fusion.106), kind=kOutput, calls=%fused_computation.143 | convolution fusion | flops 301989888 | bytes 12583936 | tf_op jit(solution)/shard_map/kab,kl->lab/dot_general | solution.py:58
  396.2 2.4 copy.55
  398.6 2.4 copy.57
  401.0 18.1 %fusion.22 = f32[16,256,384]{2,0,1:T(8,128)S(1)} fusion(f32[16,256,1]{2,0,1:T(8,128)} %copy.57, f32[16,1,384]{2,0,1:T(8,128)S(1)} %collective-permute-done.10, f32[16,256,384]{2,0,1:T(8,128)} %copy-done.6, f32[16,1,384]{2,0,1:T(8,128)S(1)} %collective-permute-done.11, f32[16,256,1]{2,0,1:T(8,128)} %copy.55, f32[16,256,384]{2,0,1:T(8,128)} %get-tuple-element.56, ...), kind=kLoop, calls=%fused_computation.26 | loop fusion | flops 40894464 | bytes 21708800 | tf_op jit(solution)/shard_map/add | solution.py:82
  419.1 2.7 copy-done.3
  421.8 10.2 %convolution_bitcast_fusion.1 = f32[16,16]{0,1:T(8,128)S(1)} fusion(f32[16,256,384]{2,0,1:T(8,128)} %get-tuple-element.56, f32[16,256,384]{2,0,1:T(8,128)S(1)} %fusion.22), kind=kOutput, calls=%fused_computation.108 | convolution fusion | flops 301989888 | bytes 12583936 | tf_op jit(solution)/shard_map/kab,lab->kl/dot_general | solution.py:54
  432.0 7.5 %psum.252 = f32[16,16]{0,1:T(8,128)S(1)} all-reduce(f32[16,16]{0,1:T(8,128)S(1)} %convolution_bitcast_fusion.1), channel_id=1, replica_groups=mesh['row_0'=4,'row_1'=2,'col_0'=4,'col_1'=4] {'row_0'}, use_global_device_ids=true, to_apply=%region_30.33 | all-reduce | flops 256 | bytes 2048 | tf_op jit(solution)/shard_map/psum | solution.py:44
  439.5 5.8 %psum.253 = f32[16,16]{0,1:T(8,128)S(1)} all-reduce(f32[16,16]{0,1:T(8,128)S(1)} %psum.252), channel_id=1, replica_groups=mesh['row_0'=4,'row_1'=2,'col_0'=4,'col_1'=4] {'row_1'}, use_global_device_ids=true, to_apply=%region_31.34 | all-reduce | flops 256 | bytes 2048 | tf_op jit(solution)/shard_map/psum | solution.py:44
  445.3 11.0 %psum.254 = f32[16,16]{0,1:T(8,128)S(1)} all-reduce(f32[16,16]{0,1:T(8,128)S(1)} %psum.253), channel_id=1, replica_groups=mesh['row_0'=4,'row_1'=2,'col_0'=4,'col_1'=4] {'col_0'}, use_global_device_ids=true, to_apply=%region_32.35 | all-reduce | flops 256 | bytes 2048 | tf_op jit(solution)/shard_map/psum | solution.py:44
  456.3 6.1 %psum.255 = f32[16,16]{0,1:T(8,128)S(1)} all-reduce(f32[16,16]{0,1:T(8,128)S(1)} %psum.254), channel_id=1, replica_groups=mesh['row_0'=4,'row_1'=2,'col_0'=4,'col_1'=4] {'col_1'}, use_global_device_ids=true, to_apply=%region_33.36 | all-reduce | flops 256 | bytes 2048 | tf_op jit(solution)/shard_map/psum | solution.py:44
  466.9 9.4 %convolution_subtract_fusion = f32[16,256,384]{2,0,1:T(8,128)S(1)} fusion(f32[16,256,384]{2,0,1:T(8,128)} %convolution_subtract_fusion.1, f32[16,16,1]{0,1,2:T(8,128)S(1)} %convolution_bitcast_fusion, f32[16,256,384]{2,0,1:T(8,128)} %copy-done.3), kind=kOutput, calls=%fused_computation.100 | convolution fusion | flops 303562752 | bytes 18875392 | tf_op jit(solution)/shard_map/kab,kl->lab/dot_general | solution.py:58
  476.3 7.6 %fusion.132 = f32[16,256,384]{2,0,1:T(8,128)S(1)} fusion(f32[16,16,1]{0,1,2:T(8,128)S(1)} %convolution_bitcast_fusion, f32[16,256,384]{2,0,1:T(8,128)} %get-tuple-element.56), kind=kOutput, calls=%fused_computation.187 | convolution fusion | flops 301989888 | bytes 12583936 | tf_op jit(solution)/shard_map/kab,kl->lab/dot_general | solution.py:58
  484.0 12.1 %add_add_fusion = f32[16,256,384]{2,0,1:T(8,128)S(1)} fusion(f32[16,256,384]{2,0,1:T(8,128)S(1)} %fusion.132, f32[16,256,384]{2,0,1:T(8,128)} %fusion.104, f32[16,256,384]{2,1,0:T(8,128)S(1)} %bitcast.146, f32[256,384]{1,0:T(8,128)S(1)} %fusion.89, f32[16,16]{1,0:T(8,128)S(1)} %fusion.117), kind=kOutput, calls=%fused_computation.80 | convolution fusion | flops 306708480 | bytes 25560064 | tf_op jit(solution)/shard_map/kab,kl->lab/dot_general | solution.py:58
  496.1 4.6 copy.62
  500.7 4.6 copy.63
  (119 shorter events, 34.0 us)
Async XLA Ops:
  0.6 16.2 %copy-start = (f32[16,256,384]{2,1,0:T(8,128)S(1)}, f32[16,256,384]{2,1,0:T(8,128)}, u32[]{:S(2)}) copy-start(f32[16,256,384]{2,1,0:T(8,128)} %param.7) | copy-start | bytes 18874372
  1.5 11.5 %collective-permute-start = (f32[1,384]{1,0:T(1,128)S(1)}, f32[1,384]{1,0:T(1,128)S(1)}, u32[]{:S(2)}, u32[]{:S(2)}) collective-permute-start(f32[1,384]{1,0:T(1,128)S(1)} %slice.108), channel_id=1, source_target_pairs={{0,16},{16,32},{32,48},{48,64},{64,80},{80,96},{96,112},{1,17},{17... | collective-permute-start | bytes 4616 | tf_op jit(solution)/shard_map/ppermute | solution.py:19
  7.7 5.3 %collective-permute-start.1 = (f32[256,1]{1,0:T(8,128)S(1)}, f32[256,1]{1,0:T(8,128)S(1)}, u32[]{:S(2)}, u32[]{:S(2)}) collective-permute-start(f32[256,1]{1,0:T(8,128)S(1)} %slice.110), channel_id=1, source_target_pairs={{0,1},{1,2},{2,3},{3,4},{4,5},{5,6},{6,7},{7,8},{8,9},{9,10},{10,1... | collective-permute-start | bytes 3080 | tf_op jit(solution)/shard_map/ppermute | solution.py:19
  20.9 2.7 copy-start.4
  25.6 49.4 %collective-permute-start.3 = (f32[16,1,384]{2,0,1:T(8,128)S(1)}, f32[16,1,384]{2,0,1:T(8,128)S(1)}, u32[]{:S(2)}, u32[]{:S(2)}) collective-permute-start(f32[16,1,384]{2,0,1:T(8,128)S(1)} %get-tuple-element.50), channel_id=1, source_target_pairs={{0,16},{16,32},{32,48},{48,64},{64,80},{80,96},{96,112},{1,17},{17... | collective-permute-start | bytes 73736 | tf_op jit(solution)/shard_map/ppermute | solution.py:30
  28.5 46.5 %collective-permute-start.2 = (f32[16,1,384]{2,0,1:T(8,128)S(1)}, f32[16,1,384]{2,0,1:T(8,128)S(1)}, u32[]{:S(2)}, u32[]{:S(2)}) collective-permute-start(f32[16,1,384]{2,0,1:T(8,128)S(1)} %get-tuple-element.51), channel_id=1, source_target_pairs={{16,0},{32,16},{48,32},{64,48},{80,64},{96,80},{112,96},{17,1},{33... | collective-permute-start | bytes 73736 | tf_op jit(solution)/shard_map/ppermute | solution.py:31
  34.0 41.0 %copy-start.7 = (f32[256,384]{1,0:T(8,128)S(1)}, f32[256,384]{1,0:T(8,128)}, u32[]{:S(2)}) copy-start(f32[256,384]{1,0:T(8,128)} %param.9) | copy-start | bytes 1179652
  34.0 38.6 %collective-permute-start.5 = (f32[16,256,1]{1,0,2:T(8,128)S(1)}, f32[16,256,1]{1,0,2:T(8,128)S(1)}, u32[]{:S(2)}, u32[]{:S(2)}) collective-permute-start(f32[16,256,1]{1,0,2:T(8,128)S(1)} %copy.32), channel_id=1, source_target_pairs={{0,1},{1,2},{2,3},{3,4},{4,5},{5,6},{6,7},{7,8},{8,9},{9,10},{10,1... | collective-permute-start | bytes 49160 | tf_op jit(solution)/shard_map/ppermute | solution.py:30
  38.3 31.9 %collective-permute-start.4 = (f32[16,256,1]{1,0,2:T(8,128)S(1)}, f32[16,256,1]{1,0,2:T(8,128)S(1)}, u32[]{:S(2)}, u32[]{:S(2)}) collective-permute-start(f32[16,256,1]{1,0,2:T(8,128)S(1)} %copy.30), channel_id=1, source_target_pairs={{1,0},{2,1},{3,2},{4,3},{5,4},{6,5},{7,6},{8,7},{9,8},{10,9},{11,1... | collective-permute-start | bytes 49160 | tf_op jit(solution)/shard_map/ppermute | solution.py:31
  72.6 30.8 %slice-start = ((s8[6291456]{0:T(1024)(128)(4,1)}), s8[2097152]{0:T(1024)(128)(4,1)S(1)}, s32[]{:S(2)}) async-start(s8[6291456]{0:T(1024)(128)(4,1)} %bitcast.143), calls=%async_computation | async-start | bytes 4194304
  75.0 28.4 %slice-start.1 = ((s8[6291456]{0:T(1024)(128)(4,1)}), s8[4194304]{0:T(1024)(128)(4,1)S(1)}, s32[]{:S(2)}) async-start(s8[6291456]{0:T(1024)(128)(4,1)} %bitcast.143), calls=%async_computation.1 | async-start | bytes 8388608
  95.3 18.8 %copy-start.1 = (f32[16,256,384]{2,0,1:T(8,128)}, f32[16,256,384]{2,0,1:T(8,128)S(1)}, u32[]{:S(2)}) copy-start(f32[16,256,384]{2,0,1:T(8,128)S(1)} %fusion.14) | copy-start | bytes 18874372
  214.3 2.7 copy-start.5
  221.1 26.1 %collective-permute-start.7 = (f32[16,1,384]{2,0,1:T(8,128)S(1)}, f32[16,1,384]{2,0,1:T(8,128)S(1)}, u32[]{:S(2)}, u32[]{:S(2)}) collective-permute-start(f32[16,1,384]{2,0,1:T(8,128)S(1)} %get-tuple-element.46), channel_id=1, source_target_pairs={{0,16},{16,32},{32,48},{48,64},{64,80},{80,96},{96,112},{1,17},{17... | collective-permute-start | bytes 73736 | tf_op jit(solution)/shard_map/ppermute | solution.py:30
  228.6 18.7 %collective-permute-start.6 = (f32[16,1,384]{2,0,1:T(8,128)S(1)}, f32[16,1,384]{2,0,1:T(8,128)S(1)}, u32[]{:S(2)}, u32[]{:S(2)}) collective-permute-start(f32[16,1,384]{2,0,1:T(8,128)S(1)} %get-tuple-element.47), channel_id=1, source_target_pairs={{16,0},{32,16},{48,32},{64,48},{80,64},{96,80},{112,96},{17,1},{33... | collective-permute-start | bytes 73736 | tf_op jit(solution)/shard_map/ppermute | solution.py:31
  235.3 9.6 %collective-permute-start.9 = (f32[16,256,1]{1,0,2:T(8,128)S(1)}, f32[16,256,1]{1,0,2:T(8,128)S(1)}, u32[]{:S(2)}, u32[]{:S(2)}) collective-permute-start(f32[16,256,1]{1,0,2:T(8,128)S(1)} %copy.45), channel_id=1, source_target_pairs={{0,1},{1,2},{2,3},{3,4},{4,5},{5,6},{6,7},{7,8},{8,9},{9,10},{10,1... | collective-permute-start | bytes 49160 | tf_op jit(solution)/shard_map/ppermute | solution.py:30
  237.6 4.8 collective-permute-start.8
  244.8 29.1 %slice-start.6 = ((s8[6291456]{0:T(1024)(128)(4,1)}), s8[2097152]{0:T(1024)(128)(4,1)S(1)}, s32[]{:S(2)}) async-start(s8[6291456]{0:T(1024)(128)(4,1)} %bitcast.149), calls=%async_computation.6 | async-start | bytes 4194304
  247.3 26.7 %slice-start.7 = ((s8[6291456]{0:T(1024)(128)(4,1)}), s8[4194304]{0:T(1024)(128)(4,1)S(1)}, s32[]{:S(2)}) async-start(s8[6291456]{0:T(1024)(128)(4,1)} %bitcast.149), calls=%async_computation.7 | async-start | bytes 8388608
  265.8 16.2 %copy-start.2 = (f32[16,256,384]{2,0,1:T(8,128)}, f32[16,256,384]{2,0,1:T(8,128)S(1)}, u32[]{:S(2)}) copy-start(f32[16,256,384]{2,0,1:T(8,128)S(1)} %fusion.34) | copy-start | bytes 18874372
  265.8 16.2 %slice-start.4 = ((s8[6291456]{0:T(1024)(128)(4,1)}), s8[4194304]{0:T(1024)(128)(4,1)S(1)}, s32[]{:S(2)}) async-start(s8[6291456]{0:T(1024)(128)(4,1)} %bitcast.147), calls=%async_computation.4 | async-start | bytes 8388608
  273.9 8.1 %slice-start.5 = ((s8[6291456]{0:T(1024)(128)(4,1)}), s8[2097152]{0:T(1024)(128)(4,1)S(1)}, s32[]{:S(2)}) async-start(s8[6291456]{0:T(1024)(128)(4,1)} %bitcast.147), calls=%async_computation.5 | async-start | bytes 4194304
  364.9 2.6 copy-start.6
  369.6 31.4 %collective-permute-start.11 = (f32[16,1,384]{2,0,1:T(8,128)S(1)}, f32[16,1,384]{2,0,1:T(8,128)S(1)}, u32[]{:S(2)}, u32[]{:S(2)}) collective-permute-start(f32[16,1,384]{2,0,1:T(8,128)S(1)} %get-tuple-element.42), channel_id=1, source_target_pairs={{0,16},{16,32},{32,48},{48,64},{64,80},{80,96},{96,112},{1,17},{17... | collective-permute-start | bytes 73736 | tf_op jit(solution)/shard_map/ppermute | solution.py:30
  378.5 22.5 %collective-permute-start.10 = (f32[16,1,384]{2,0,1:T(8,128)S(1)}, f32[16,1,384]{2,0,1:T(8,128)S(1)}, u32[]{:S(2)}, u32[]{:S(2)}) collective-permute-start(f32[16,1,384]{2,0,1:T(8,128)S(1)} %get-tuple-element.43), channel_id=1, source_target_pairs={{16,0},{32,16},{48,32},{64,48},{80,64},{96,80},{112,96},{17,1},{33... | collective-permute-start | bytes 73736 | tf_op jit(solution)/shard_map/ppermute | solution.py:31
  384.0 16.9 %copy-start.8 = (f32[256,384]{1,0:T(8,128)S(1)}, f32[256,384]{1,0:T(8,128)}, u32[]{:S(2)}) copy-start(f32[256,384]{1,0:T(8,128)} %param.8) | copy-start | bytes 1179652
  384.0 16.9 %copy-start.9 = (f32[256,384]{1,0:T(8,128)S(1)}, f32[256,384]{1,0:T(8,128)}, u32[]{:S(2)}) copy-start(f32[256,384]{1,0:T(8,128)} %convert_element_type.10) | copy-start | bytes 1179652
  384.0 16.9 %copy-start.10 = (f32[256,384]{1,0:T(8,128)S(1)}, f32[256,384]{1,0:T(8,128)}, u32[]{:S(2)}) copy-start(f32[256,384]{1,0:T(8,128)} %get-tuple-element.36) | copy-start | bytes 1179652
  384.0 17.0 %copy-start.11 = (f32[256,384]{1,0:T(8,128)S(1)}, f32[256,384]{1,0:T(8,128)}, u32[]{:S(2)}) copy-start(f32[256,384]{1,0:T(8,128)} %get-tuple-element.38) | copy-start | bytes 1179652
  384.0 17.0 %copy-start.12 = (f32[256,384]{1,0:T(8,128)S(1)}, f32[256,384]{1,0:T(8,128)}, u32[]{:S(2)}) copy-start(f32[256,384]{1,0:T(8,128)} %get-tuple-element.39) | copy-start | bytes 1179652
  384.0 14.5 %collective-permute-start.13 = (f32[16,256,1]{1,0,2:T(8,128)S(1)}, f32[16,256,1]{1,0,2:T(8,128)S(1)}, u32[]{:S(2)}, u32[]{:S(2)}) collective-permute-start(f32[16,256,1]{1,0,2:T(8,128)S(1)} %copy.56), channel_id=1, source_target_pairs={{0,1},{1,2},{2,3},{3,4},{4,5},{5,6},{6,7},{7,8},{8,9},{9,10},{10,1... | collective-permute-start | bytes 49160 | tf_op jit(solution)/shard_map/ppermute | solution.py:30
  385.5 10.7 %collective-permute-start.12 = (f32[16,256,1]{1,0,2:T(8,128)S(1)}, f32[16,256,1]{1,0,2:T(8,128)S(1)}, u32[]{:S(2)}, u32[]{:S(2)}) collective-permute-start(f32[16,256,1]{1,0,2:T(8,128)S(1)} %copy.54), channel_id=1, source_target_pairs={{1,0},{2,1},{3,2},{4,3},{5,4},{6,5},{7,6},{8,7},{9,8},{10,9},{11,1... | collective-permute-start | bytes 49160 | tf_op jit(solution)/shard_map/ppermute | solution.py:31
  419.1 2.7 copy-start.3
  421.8 62.1 %slice-start.2 = ((s8[6291456]{0:T(1024)(128)(4,1)}), s8[2097152]{0:T(1024)(128)(4,1)S(1)}, s32[]{:S(2)}) async-start(s8[6291456]{0:T(1024)(128)(4,1)} %bitcast.145), calls=%async_computation.2 | async-start | bytes 4194304
  466.9 17.0 %slice-start.3 = ((s8[6291456]{0:T(1024)(128)(4,1)}), s8[4194304]{0:T(1024)(128)(4,1)S(1)}, s32[]{:S(2)}) async-start(s8[6291456]{0:T(1024)(128)(4,1)} %bitcast.145), calls=%async_computation.3 | async-start | bytes 8388608
where the time goes:
time: 515 us; the launch traced here: 505 us
  matrix products  186 us (36%)
  blocking collectives  129 us (25%)
  other arithmetic  86.4 us (17%)
  local copies, waits for them, and re-layouts  53.4 us (10%)
  starting transfers between devices  46.9 us (9%)
    psum x12, blocking collectives, one_axis_at_a_time(): shard = lax.psum(shard, axis)  129 us
    dot_general x8, matrix products, gram(): return jnp.einsum('kab,lab->kl', left, right, precision=exact_precision)  94.3 us
    dot_general x8, matrix products, combine(): return jnp.einsum('kab,kl->lab', field, matrix, precision=exact_precision)  88.5 us
    add x3, other arithmetic, shards(): pad_nodes * direction  56.9 us
    ppermute x6, starting transfers between devices, with_halo(): lax.ppermute(last, axis, up)  27.2 us
    unnamed x44, local copies, waits for them, and re-layouts  20 us
    slice x6, local copies, waits for them, and re-layouts, with_halo(): first = lax.slice_in_dim(shard, 0, width, axis=dim)  13.6 us
    ppermute x6, starting transfers between devices, with_halo(): lax.ppermute(first, axis, [(b, a) for a, b in up])  11.3 us
  transfers between devices with their start and end apart: 14, of which 2 were waited for; matrix products, arithmetic and copies ran while one was open for 14% of the time, Pallas kernels for 0%

commit v1 on v0

v1 whole, which is shorter than its diff:
```python
import functools

import jax
import jax.numpy as jnp
from jax import lax
from jax.experimental import pallas as pl
from jax.experimental.pallas import tpu as pltpu
from jax.sharding import PartitionSpec as P

RHS = 16
STEPS = 3
LANES = 128
MESH = pl.DeviceIdType.MESH
F32 = jnp.float32
BF16 = jnp.bfloat16
UNROLL = 8
GROUP = 64
ROWS = 32


def split(value):
    high = value.astype(BF16)
    return high, (value - high.astype(F32)).astype(BF16)


def lane_of(shape):
    return lax.broadcasted_iota(jnp.int32, shape, len(shape) - 1)


def tiles_of(value):
    return [value[:, c : c + LANES] for c in range(0, value.shape[1], LANES)]


def stay_scalar(flag):
    return jnp.where(flag, 1.0, 0.0).astype(F32)


def gram_dot(left, right):
    return lax.dot_general(left, right, (((1,), (1,)), ((), ())), preferred_element_type=F32)


def eliminate(stack, order):
    rows = stack.shape[0]
    lane = lane_of((1, LANES))
    start = 0
    for p in range(order):
        keep = p // 8 * 8
        if keep > start:
            stack = stack[keep - start :]
            start = keep
        row = stack[p - start : p - start + 1, :]
        pivot = row[:, p : p + 1]
        col = stack[:, p : p + 1] / pivot
        stack = jnp.where(lane == p, col, stack - col * row)
    return stack[order - start :]


def main_kernel(grid, rhs, cx_in, cy_in, pad_in, ub0, ub1, ub2, ub3, lhs, dm, dp,
                cx, cy, pad, s, u0, u1, u2, bx, by, natural, byl, pk, cyh, sh, upk, uh, gsend, ga, gb,
                in_sem, bar_send, bar_recv):
    nrow, ncol = grid
    rb, cb = dm.shape
    nb = rb // LANES
    row, col = lax.axis_index("row"), lax.axis_index("col")
    down, above = lax.rem(row + 1, nrow), lax.rem(row + nrow - 1, nrow)
    right, left = lax.rem(col + 1, ncol), lax.rem(col + ncol - 1, ncol)
    fields = [u0, u1, u2]
    basis = [ub0, ub1, ub2, ub3]
    used = [0]
    sent = []

    def send(src, dst, row_to, col_to):
        slot = used[0]
        used[0] += 1
        copy = pltpu.make_async_remote_copy(
            src_ref=src, dst_ref=dst, send_sem=bar_send.at[slot], recv_sem=bar_recv.at[slot],
            device_id=(row_to, col_to), device_id_type=MESH)
        copy.start()
        sent.append(copy)
        return copy

    local = []
    for n, (src, dst) in enumerate(((cy_in, cy), (cx_in, cx.at[pl.ds(8, rb)]), (pad_in, pad))):
        copy = pltpu.make_async_copy(src, dst, in_sem.at[n])
        copy.start()
        local.append(copy)
    fill = []
    for k in range(RHS):
        copy = pltpu.make_async_copy(rhs.at[k], u0.at[pl.ds(1, rb), k, :], in_sem.at[3 + k])
        copy.start()
        fill.append(copy)

    barrier = pltpu.get_barrier_semaphore()
    for d in range(1, nrow):
        pl.semaphore_signal(barrier, inc=1, device_id=(lax.rem(row + d, nrow), col), device_id_type=MESH)
    for d in range(1, ncol):
        pl.semaphore_signal(barrier, inc=1, device_id=(row, lax.rem(col + d, ncol)), device_id_type=MESH)

    local[0].wait()
    pk[0] = jnp.transpose(cy[:, cb - LANES :])[LANES - 8 :]
    local[1].wait()
    pl.semaphore_wait(barrier, nrow + ncol - 2)
    got_cx = send(cx.at[pl.ds(rb, 8)], cx.at[pl.ds(0, 8)], down, col)
    got_cy = send(pk.at[0], cyh, row, right)
    local[2].wait()
    got_cx.wait_recv()
    got_cy.wait_recv()
    cx[0:8] = cx[0:8] * stay_scalar(row > 0)
    cyh[...] = cyh[...] * stay_scalar(col > 0)
    natural[...] = jnp.transpose(jnp.broadcast_to(cyh[7:8, :], (LANES, rb)))
    chunk = 32
    for r in range(0, rb, chunk):
        here = pl.ds(r, chunk)
        cond_y = cy[here]
        rolled = pltpu.roll(cond_y, 1, axis=1)
        first = jnp.where(lane_of((chunk, LANES)) == 0, natural[here], rolled[:, :LANES])
        cond_left = jnp.concatenate([first, rolled[:, LANES:]], axis=1)
        pads = pad[here].astype(F32)
        free = 1.0 - pads
        diagonal = free * (cx[pl.ds(r + 8, chunk)] + cx[pl.ds(r + 7, chunk)] + cond_y + cond_left) + pads
        root = lax.rsqrt(diagonal)
        dm[here] = root
        dp[here] = diagonal * root
        s[pl.ds(r + 8, chunk)] = free * root
    pk[1] = jnp.transpose(s[pl.ds(8, rb), 0:LANES])[:8]
    pk[2] = jnp.transpose(s[pl.ds(8, rb), cb - LANES : cb])[LANES - 8 :]
    got_s = [
        send(s.at[pl.ds(rb, 8)], s.at[pl.ds(0, 8)], down, col),
        send(s.at[pl.ds(8, 8)], s.at[pl.ds(rb + 8, 8)], above, col),
        send(pk.at[1], sh.at[1], row, left),
        send(pk.at[2], sh.at[0], row, right),
    ]

    def send_edges(j):
        field = fields[j]
        return [
            send(field.at[rb], field.at[0], down, col),
            send(field.at[1], field.at[rb + 1], above, col),
            send(upk.at[j, 0], uh.at[j, 1], row, left),
            send(upk.at[j, 1], uh.at[j, 0], row, right),
        ]

    lane = lane_of((RHS, LANES))

    def store_split(j, r, value):
        high, low = split(value)
        basis[j][r, :RHS, :] = high
        basis[j][r, RHS:, :] = low

    def pack_edges(value, r, held):
        low, high = held
        low = jnp.where(lane == r, pltpu.roll(value[:, :LANES], r, axis=1), low)
        high = jnp.where(lane == r, pltpu.roll(value[:, cb - LANES :], lax.rem(r + 1, LANES), axis=1), high)
        return low, high

    empty = (jnp.zeros((RHS, LANES), F32), jnp.zeros((RHS, LANES), F32))

    for copy in fill:
        copy.wait()
    for b in range(nb):
        def begin(i, held, b=b):
            for t in range(UNROLL):
                r = i * UNROLL + t
                at = b * LANES + r
                value = u0[at + 1] * dm[pl.ds(at, 1), :]
                u0[at + 1] = value
                store_split(0, at, value)
                held = pack_edges(value, r, held)
            return held

        low, high = lax.fori_loop(0, LANES // UNROLL, begin, empty)
        upk[0, 0, b] = low
        upk[0, 1, b] = high
    got_u = send_edges(0)

    lows = STEPS + 1

    def gram_loop(left_blocks, right_blocks):
        height = len(left_blocks) * RHS
        width = len(right_blocks) * RHS

        def body(i, total):
            rows = [i * GROUP + t for t in range(GROUP)]

            def operand(blocks):
                parts = [
                    jnp.concatenate(
                        [basis[n % lows][r, n // lows * RHS : (n // lows + 1) * RHS, :] for n in blocks], axis=0)
                    for r in rows
                ]
                return jnp.concatenate(parts, axis=1)

            return total + gram_dot(operand(left_blocks), operand(right_blocks))

        return lax.fori_loop(0, rb // GROUP, body, jnp.zeros((height, width), F32))

    def keep_moment(k, value):
        gsend[0, :, k * RHS : (k + 1) * RHS] = value

    gsend[...] = jnp.zeros_like(gsend)
    total = gram_loop([0], [0, lows])
    keep_moment(0, total[:, :RHS] + 2.0 * total[:, RHS:])

    for copy in got_s:
        copy.wait_recv()
    s[pl.ds(rb + 8, 8)] = s[pl.ds(rb + 8, 8)] * stay_scalar(row < nrow - 1)
    sh[1] = sh[1] * stay_scalar(col < ncol - 1)
    byl[...] = jnp.broadcast_to(cyh[7:8, :] * sh[0, 7:8, :] * pk[1, 0:1, :], (8, rb))
    natural[...] = jnp.transpose(jnp.broadcast_to(sh[1, 0:1, :], (LANES, rb)))
    for r in range(0, rb, chunk):
        here = pl.ds(r, chunk)
        mine = s[pl.ds(r + 8, chunk)]
        rolled = pltpu.roll(mine, cb - 1, axis=1)
        last = jnp.where(lane_of((chunk, LANES)) == LANES - 1, natural[here], rolled[:, cb - LANES :])
        following = jnp.concatenate([rolled[:, : cb - LANES], last], axis=1)
        by[here] = cy[here] * mine * following
        bx[here] = cx[pl.ds(r + 7, chunk)] * s[pl.ds(r + 7, chunk)] * mine
    bx[rb : rb + 1] = cx[rb + 7 : rb + 8] * s[rb + 7 : rb + 8] * s[rb + 8 : rb + 9]

    for j in range(STEPS):
        for copy in got_u:
            copy.wait_recv()
        source = fields[j]
        final = j == STEPS - 1
        for b in range(nb):
            from_left = uh[j, 0, b] * byl[0:1, b * LANES : (b + 1) * LANES]
            from_right = uh[j, 1, b]

            def apply(i, held, b=b, from_left=from_left, from_right=from_right, source=source, j=j, final=final):
                for t in range(UNROLL):
                    r = i * UNROLL + t
                    at = b * LANES + r
                    here = source[at + 1]
                    side = by[pl.ds(at, 1), :]
                    total = bx[pl.ds(at, 1), :] * source[at] + bx[pl.ds(at + 1, 1), :] * source[at + 2]
                    ahead = [pltpu.roll(v, LANES - 1, axis=1) for v in tiles_of(here)]
                    ahead.append(pltpu.roll(from_right, LANES - 1 - r, axis=1))
                    ahead = [jnp.where(lane == LANES - 1, ahead[c + 1], ahead[c]) for c in range(len(ahead) - 1)]
                    behind = [pltpu.roll(v, 1, axis=1) for v in tiles_of(side * here)]
                    behind.insert(0, pltpu.roll(from_left, lax.rem(LANES - r, LANES), axis=1))
                    behind = [jnp.where(lane == 0, behind[c], behind[c + 1]) for c in range(len(behind) - 1)]
                    value = total + side * jnp.concatenate(ahead, axis=1) + jnp.concatenate(behind, axis=1)
                    store_split(j + 1, at, value)
                    if not final:
                        fields[j + 1][at + 1] = value
                        held = pack_edges(value, r, held)
                return held

            low, high = lax.fori_loop(0, LANES // UNROLL, apply, empty)
            if not final:
                upk[j + 1, 0, b] = low
                upk[j + 1, 1, b] = high
        if not final:
            got_u = send_edges(j + 1)
            total = gram_loop([j, lows + j, j + 1], [j + 1, lows + j + 1])
            even = total[2 * RHS :]
            keep_moment(2 * j + 2, even[:, :RHS] + 2.0 * even[:, RHS:])
        else:
            total = gram_loop([j, lows + j], [j + 1, lows + j + 1])
        keep_moment(2 * j + 1, total[:RHS, :RHS] + total[:RHS, RHS:] + total[RHS : 2 * RHS, :RHS])

    def reduce_over(size, me, slots, n, place):
        got = []
        for d in range(1, size):
            to = lax.rem(me + d, size)
            got.append(send(gsend.at[n], slots.at[me], *place(to)))
        slots[me] = gsend[n]
        for copy in got:
            copy.wait_recv()
        total = slots[0]
        for n in range(1, size):
            total = total + slots[n]
        return total

    gsend[1] = reduce_over(nrow, row, ga, 0, lambda to: (to, col))
    total = reduce_over(ncol, col, gb, 1, lambda to: (row, to))

    wide = lane_of((RHS, LANES))
    turned = jnp.transpose(total)
    turned = jnp.concatenate([turned[k * RHS : (k + 1) * RHS] for k in range(LANES // RHS)], axis=1)
    moments = 0.5 * (total + turned)
    stiff = moments - pltpu.roll(moments, LANES - RHS, axis=1)
    order = STEPS * RHS
    blocks = [stiff] + [pltpu.roll(stiff, LANES - RHS * n, axis=1) for n in range(1, STEPS)] + [moments]
    stack = jnp.concatenate([jnp.where(wide < order, v, 0.0) for v in blocks], axis=0)
    solved = eliminate(stack, order)
    unit = jnp.where(wide == lax.broadcasted_iota(jnp.int32, (RHS, LANES), 0), 1.0, 0.0)
    remain = unit - solved + pltpu.roll(solved, RHS, axis=1)
    coef = jnp.concatenate([solved, remain], axis=0)
    high = coef.astype(BF16).astype(F32)
    low = coef - high
    lhs[...] = jnp.concatenate([high + pltpu.roll(high, LANES // 2, axis=1), low], axis=0).astype(BF16)

    for copy in sent:
        copy.wait_send()


def combine_kernel(ub0, ub1, ub2, ub3, lhs, dm, dp, x_out, r_out, x_buf, r_buf, sem):
    rb, cb = dm.shape
    block = 64
    coef = lhs[...]
    started = []
    for n in range(rb // block):
        def body(i, carry, n=n):
            rows = [n * block + i * ROWS + t for t in range(ROWS)]
            out = jnp.dot(coef, jnp.concatenate(
                [
                    jnp.concatenate([v[r, m : m + RHS, :] for m in (0, RHS) for v in (ub0, ub1, ub2, ub3)], axis=0)
                    for r in rows
                ], axis=1), preferred_element_type=F32)
            for t, r in enumerate(rows):
                part = out[:, t * cb : (t + 1) * cb]
                x_buf[r] = (part[:RHS] + part[2 * RHS : 3 * RHS]) * dm[pl.ds(r, 1), :]
                r_buf[r] = (part[RHS : 2 * RHS] + part[3 * RHS :]) * dp[pl.ds(r, 1), :]
            return carry

        lax.fori_loop(0, block // ROWS, body, 0)
        here = pl.ds(n * block, block)
        for k in range(RHS):
            for m, (buf, out) in enumerate(((x_buf, x_out), (r_buf, r_out))):
                copy = pltpu.make_async_copy(buf.at[here, k, :], out.at[k, here, :], sem.at[n, m, k])
                copy.start()
                started.append(copy)
    for copy in started:
        copy.wait()


def shards(nrow, ncol, right_side, cond_x, cond_y, pad_mask):
    rb, cb = cond_x.shape
    nb = rb // LANES
    sends = 2 + 4 + 4 * STEPS + (nrow - 1) + (ncol - 1)
    hbm = pl.BlockSpec(memory_space=pltpu.HBM)
    vmem = pl.BlockSpec(memory_space=pltpu.VMEM)
    field = pltpu.VMEM((rb + 2, RHS, cb), F32)
    *kept, = pl.pallas_call(
        functools.partial(main_kernel, (nrow, ncol)),
        out_shape=(
            *[pltpu.VMEM((rb, 2 * RHS, cb), BF16)] * (STEPS + 1), pltpu.VMEM((4 * RHS, LANES), BF16),
            pltpu.VMEM((rb, cb), F32), pltpu.VMEM((rb, cb), F32),
        ),
        in_specs=[hbm] * 4,
        out_specs=(vmem,) * (STEPS + 4),
        scratch_shapes=[
            pltpu.VMEM((rb + 8, cb), F32), pltpu.VMEM((rb, cb), F32), pltpu.VMEM((rb, cb), jnp.int32),
            pltpu.VMEM((rb + 16, cb), F32), field, field, field,
            pltpu.VMEM((rb + 8, cb), F32), pltpu.VMEM((rb, cb), F32),
            pltpu.VMEM((rb, LANES), F32), pltpu.VMEM((8, rb), F32), pltpu.VMEM((3, 8, rb), F32),
            pltpu.VMEM((8, rb), F32), pltpu.VMEM((2, 8, rb), F32),
            pltpu.VMEM((STEPS, 2, nb, RHS, LANES), F32), pltpu.VMEM((STEPS, 2, nb, RHS, LANES), F32),
            pltpu.VMEM((2, RHS, LANES), F32), pltpu.VMEM((nrow, RHS, LANES), F32), pltpu.VMEM((ncol, RHS, LANES), F32),
            pltpu.SemaphoreType.DMA((3 + RHS,)), pltpu.SemaphoreType.DMA((sends,)), pltpu.SemaphoreType.DMA((sends,)),
        ],
        compiler_params=pltpu.CompilerParams(
            collective_id=0, has_side_effects=True, vmem_limit_bytes=24 * 2**20),
    )(*(pltpu.with_memory_space_constraint(v, pltpu.HBM) for v in (right_side, cond_x, cond_y, pad_mask)))
    out = jax.ShapeDtypeStruct((RHS, rb, cb), F32)
    return pl.pallas_call(
        combine_kernel,
        out_shape=(out, out),
        in_specs=[vmem] * (STEPS + 4),
        out_specs=(hbm, hbm),
        scratch_shapes=[
            pltpu.VMEM((rb, RHS, cb), F32), pltpu.VMEM((rb, RHS, cb), F32),
            pltpu.SemaphoreType.DMA((rb // 64, 2, RHS)),
        ],
        compiler_params=pltpu.CompilerParams(vmem_limit_bytes=14 * 2**20),
    )(*kept)


def solution(mesh):
    nrow, ncol = mesh.shape["row"], mesh.shape["col"]
    field, plane = P(None, "row", "col"), P("row", "col")
    return jax.shard_map(
        functools.partial(shards, nrow, ncol), mesh=mesh,
        in_specs=(field, plane, plane, plane), out_specs=(field, field), check_vma=False,
    )
```

time: 515 us -> 85.5 us (0.17); the launches traced: 505 us -> 85.4 us
  matrix products: 186 us -> 0 us
  blocking collectives: 129 us -> 0 us
  other arithmetic: 86.4 us -> 0 us
  Pallas kernels: 0 us -> 84.8 us
  local copies, waits for them, and re-layouts: 53.4 us -> 0 us
  starting transfers between devices: 46.9 us -> 0 us
    dot_general x22 -> x0, matrix products: 184 us -> none  [the longest x8 94.3 us: gram(): return jnp.einsum('kab,lab->kl', left, right, precision=exact_precision)]
    psum x12 -> x0, blocking collectives: 129 us -> none  [one_axis_at_a_time(): shard = lax.psum(shard, axis)]
    pallas_call x0 -> x2, Pallas kernels: none -> 84.8 us  [the longest x1 76.9 us: shards(): pl.pallas_call(functools.partial(main_kernel, (nrow, ncol)), out_shape=(*...]
    add x4 -> x0, other arithmetic: 59.6 us -> none  [the longest x3 56.9 us: shards(): pad_nodes * direction]
    ppermute x14 -> x0, starting transfers between devices: 46.9 us -> none  [the longest x6 27.2 us: with_halo(): lax.ppermute(last, axis, up)]
    unnamed x44 -> x0, local copies, waits for them, and re-layouts: 20 us -> none
    another operation x25 -> x0, other arithmetic: 19.8 us -> none  [the longest x15 10.7 us: small_solve(): factor = jnp.linalg.cholesky(matrix)]
    slice x14 -> x0, local copies, waits for them, and re-layouts: 18.5 us -> none  [the longest x6 13.6 us: with_halo(): first = lax.slice_in_dim(shard, 0, width, axis=dim)]
  transfers between devices with their start and end apart: 14 -> 0, of which waited for: 2 -> 0; matrix products, arithmetic and copies ran while one was open for 14% -> 0% of each run, Pallas kernels for 0% -> 0%
where the time goes in v1:
time: 85.5 us; the launch traced here: 85.4 us
  Pallas kernels  84.8 us (99%)
    pallas_call x1, Pallas kernels, shards(): pl.pallas_call(functools.partial(main_kernel, (nrow, ncol)), out_shape=(*...  76.9 us
    pallas_call x1, Pallas kernels, shards(): pl.pallas_call(combine_kernel, out_shape=(out, out), in_specs=[vmem] * (S...  7.87 us

profile of v1, /device:TPU:1, one launch (start us, length us, event | category | flops | bytes accessed | tf_op | source)
XLA Modules:
  0.0 85.4 jit_solution(5939318021523432602)
XLA Ops:
  0.6 76.9 %shard_map.59 = (bf16[256,32,384]{2,1,0:T(8,128)(2,1)S(1)}, bf16[256,32,384]{2,1,0:T(8,128)(2,1)S(1)}, bf16[256,32,384]{2,1,0:T(8,128)(2,1)S(1)}, bf16[256,32,38...) custom-call(f32[16,256,384]{2,1,0:T(8,128)} %rhs.1, ...), custom_call_target="tpu_custom_call" | custom-call | tf_op jit(solution)/shard_map/pallas_call | solution.py:335
  77.6 7.9 %shard_map.60 = (f32[16,256,384]{2,1,0:T(8,128)}, f32[16,256,384]{2,1,0:T(8,128)}) custom-call(bf16[256,32,384]{2,1,0:T(8,128)(2,1)S(1)} %get-tuple-element.9.ub0, bf16[256,32,384]{2,1,0:T(8,128)(2,1)S(1)} %get-tuple-element.10.ub1, bf16[256,32,384]{2,1,0:T(8,128)(2,1)S(1)} %get-tuple-element.11.ub2, bf16[256,32,384]{2,1,0:T(8,128)(2,1)S(1)} %get-tuple-element.12.ub3, ...), custom_call_target="tpu_custom_call" | custom-call | tf_op jit(solution)/shard_map/pallas_call | solution.py:357

commit v2 on v1

v2 whole, which is shorter than its diff:
```python
import functools

import jax
import jax.numpy as jnp
from jax import lax
from jax.experimental import pallas as pl
from jax.experimental.pallas import tpu as pltpu
from jax.sharding import PartitionSpec as P

RHS = 16
STEPS = 3
LANES = 128
MESH = pl.DeviceIdType.MESH
F32 = jnp.float32
BF16 = jnp.bfloat16
UNROLL = 16
BEGIN = 16
SHIFT = 64
GROUP = 64
ROWS = 64


def split(value):
    high = value.astype(BF16)
    return high, (value - high.astype(F32)).astype(BF16)


def lane_of(shape):
    return lax.broadcasted_iota(jnp.int32, shape, len(shape) - 1)


def tiles_of(value):
    return [value[:, c : c + LANES] for c in range(0, value.shape[1], LANES)]


def stay_scalar(flag):
    return jnp.where(flag, 1.0, 0.0).astype(F32)


def gram_dot(left, right):
    return lax.dot_general(left, right, (((1,), (1,)), ((), ())), preferred_element_type=F32)


def eliminate(stack, order, first):
    rows = stack.shape[0]
    lane = lane_of((1, LANES))
    start = 0
    for p in range(order):
        keep = p // 8 * 8
        if keep > start:
            stack = stack[keep - start :]
            start = keep
        row = stack[p - start : p - start + 1, :]
        at = first + p
        col = stack[:, at : at + 1] / row[:, at : at + 1]
        stack = jnp.where(lane == at, col, stack - col * row)
    return stack[order - start :]


def main_kernel(grid, rhs, cx_in, cy_in, pad_in, ub0, ub1, ub2, ub3, lhs, dm, dp, cxh,
                cx, cy, pad, s, u0, u1, bx, by, bys, natural, pk, cyh, sh, upk, uh, edge, rolled, turn, gsend, ga, gb,
                in_sem, bar_send, bar_recv):
    nrow, ncol = grid
    rb, cb = dm.shape
    nb = rb // LANES
    row, col = lax.axis_index("row"), lax.axis_index("col")
    down, above = lax.rem(row + 1, nrow), lax.rem(row + nrow - 1, nrow)
    right, left = lax.rem(col + 1, ncol), lax.rem(col + ncol - 1, ncol)
    fields = [u0, u1, u0]
    basis = [ub0, ub1, ub2, ub3]
    used = [0]
    sent = []

    def send(src, dst, row_to, col_to):
        slot = used[0]
        used[0] += 1
        copy = pltpu.make_async_remote_copy(
            src_ref=src, dst_ref=dst, send_sem=bar_send.at[slot], recv_sem=bar_recv.at[slot],
            device_id=(row_to, col_to), device_id_type=MESH)
        copy.start()
        sent.append(copy)
        return copy

    def done(copy):
        copy.wait_send()
        sent[:] = [c for c in sent if c is not copy]

    barrier = pltpu.get_barrier_semaphore()
    for d in range(1, nrow):
        pl.semaphore_signal(barrier, inc=1, device_id=(lax.rem(row + d, nrow), col), device_id_type=MESH)
    for d in range(1, ncol):
        pl.semaphore_signal(barrier, inc=1, device_id=(row, lax.rem(col + d, ncol)), device_id_type=MESH)

    local = []
    for n, (src, dst) in enumerate(((cy_in, cy), (cx_in, cx.at[pl.ds(8, rb)]), (pad_in, pad))):
        copy = pltpu.make_async_copy(src, dst, in_sem.at[n])
        copy.start()
        local.append(copy)
    fill = []
    for k in range(RHS):
        copy = pltpu.make_async_copy(rhs.at[k], u0.at[pl.ds(1, rb), k, :], in_sem.at[3 + k])
        copy.start()
        fill.append(copy)

    local[0].wait()
    pk[0] = jnp.transpose(cy[:, cb - LANES :])[LANES - 8 :]
    local[1].wait()
    pl.semaphore_wait(barrier, nrow + ncol - 2)
    got_cx = send(cx.at[pl.ds(rb, 8)], cxh, down, col)
    got_cy = send(pk.at[0], cyh, row, right)
    local[2].wait()
    cx[0:8] = jnp.zeros_like(cxh)
    chunk = 32

    def scale_nodes(r, height, width, left_known):
        here = pl.ds(r, height)
        cond_y = cy[here, :width]
        moved = pltpu.roll(cond_y, 1, axis=1)
        if left_known:
            first = jnp.where(lane_of((height, LANES)) == 0, natural[0, here], moved[:, :LANES])
            moved = jnp.concatenate([first, moved[:, LANES:]], axis=1) if width > LANES else first
        pads = pad[here, :width].astype(F32)
        free = 1.0 - pads
        diagonal = free * (cx[pl.ds(r + 8, height), :width] + cx[pl.ds(r + 7, height), :width] + cond_y + moved) + pads
        root = lax.rsqrt(diagonal)
        dm[here, :width] = root
        dp[here, :width] = diagonal * root
        s[pl.ds(r + 8, height), :width] = free * root

    for r in range(0, rb, chunk):
        scale_nodes(r, chunk, cb, False)

    lane = lane_of((RHS, LANES))

    def store_split(j, r, value, start=0):
        high, low = split(value)
        lanes = slice(start, start + value.shape[1])
        basis[j][r, :RHS, lanes] = high
        basis[j][r, RHS:, lanes] = low

    for copy in fill:
        copy.wait()
    rolled[0, 0] = u0[1]

    def inner(i, carry):
        for t in range(BEGIN):
            at = i * BEGIN + t
            value = u0[at + 1, :, LANES:] * dm[pl.ds(at, 1), :][:, LANES:]
            u0[at + 1, :, LANES:] = value
            store_split(0, at, value, LANES)
        return carry

    lax.fori_loop(0, rb // BEGIN, inner, 0)

    got_cx.wait_recv()
    got_cy.wait_recv()
    cx[0:8] = cxh[...] * stay_scalar(row > 0)
    cyh[...] = cyh[...] * stay_scalar(col > 0)
    natural[0] = jnp.transpose(jnp.broadcast_to(cyh[7:8, :], (LANES, rb)))
    scale_nodes(0, 8, cb, True)
    for r in range(0, rb, chunk):
        scale_nodes(r, chunk, LANES, True)
    pk[1] = jnp.transpose(s[pl.ds(8, rb), 0:LANES])[:8]
    pk[2] = jnp.transpose(s[pl.ds(8, rb), cb - LANES : cb])[LANES - 8 :]
    got_s = [
        send(s.at[pl.ds(rb, 8)], s.at[pl.ds(0, 8)], down, col),
        send(s.at[pl.ds(8, 8)], s.at[pl.ds(rb + 8, 8)], above, col),
        send(pk.at[1], sh.at[1], row, left),
        send(pk.at[2], sh.at[0], row, right),
    ]

    def send_edges(j):
        field = fields[j]
        return [
            send(field.at[rb], edge.at[j, 0], down, col),
            send(field.at[1], edge.at[j, 1], above, col),
            send(upk.at[j, 0], uh.at[j, 1], row, left),
            send(upk.at[j, 1], uh.at[j, 0], row, right),
        ]

    even_lane = (lane & 1) == 0

    def pack_edges(first, last, r, parity, held):
        ends = pltpu.roll(jnp.where(lane == LANES - 1, last, first), r, axis=1)
        here = (lane == r) | (lane == ((r - 1) & (LANES - 1)))
        return tuple(jnp.where(here, ends, held[n]) if n == parity else held[n] for n in range(2))

    def keep_edges(j, b, held):
        upk[j, 0, b] = jnp.where(even_lane, held[0], held[1])
        upk[j, 1, b] = jnp.where(even_lane, held[1], held[0])

    empty = (jnp.zeros((RHS, LANES), F32), jnp.zeros((RHS, LANES), F32))

    top = rolled[0, 0] * dm[0:1, :]
    u0[1, :, LANES:] = top[:, LANES:]
    store_split(0, 0, top[:, LANES:], LANES)
    for b in range(nb):
        def begin(i, held, b=b):
            for t in range(BEGIN):
                r = i * BEGIN + t
                at = b * LANES + r
                value = u0[at + 1, :, :LANES] * dm[pl.ds(at, 1), :][:, :LANES]
                u0[at + 1, :, :LANES] = value
                store_split(0, at, value)
                held = pack_edges(value, u0[at + 1, :, cb - LANES :], r, t % 2, held)
            return held

        keep_edges(0, b, lax.fori_loop(0, LANES // BEGIN, begin, empty))
    got_u = send_edges(0)

    lows = STEPS + 1

    def gram_loop(left_blocks, right_blocks):
        height = len(left_blocks) * RHS
        width = len(right_blocks) * RHS

        def body(i, total):
            rows = [i * GROUP + t for t in range(GROUP)]

            def operand(blocks):
                parts = [
                    jnp.concatenate(
                        [basis[n % lows][r, n // lows * RHS : (n // lows + 1) * RHS, :] for n in blocks], axis=0)
                    for r in rows
                ]
                return jnp.concatenate(parts, axis=1)

            return total + gram_dot(operand(left_blocks), operand(right_blocks))

        return lax.fori_loop(0, rb // GROUP, body, jnp.zeros((height, width), F32))

    def keep_moment(k, value):
        gsend[0 if k < 2 * STEPS - 1 else 2, :, k * RHS : (k + 1) * RHS] = value

    gsend[...] = jnp.zeros_like(gsend)
    place = lax.broadcasted_iota(jnp.int32, turn.shape, 0) & (LANES - 1)
    spot = lane_of(turn.shape)
    comes = jnp.where(spot < LANES, spot + 1, spot - 1) & (LANES - 1)
    turn[...] = jnp.where(place == comes, 1.0, 0.0).astype(BF16)
    total = gram_loop([0], [0, lows])
    keep_moment(0, total[:, :RHS] + 2.0 * total[:, RHS:])

    for copy in got_s:
        copy.wait_recv()
    s[pl.ds(rb + 8, 8)] = s[pl.ds(rb + 8, 8)] * stay_scalar(row < nrow - 1)
    sh[1] = sh[1] * stay_scalar(col < ncol - 1)
    natural[1] = jnp.transpose(jnp.broadcast_to(sh[0, 7:8, :], (LANES, rb)))
    natural[2] = jnp.transpose(jnp.broadcast_to(sh[1, 0:1, :], (LANES, rb)))
    for r in range(0, rb, chunk):
        here = pl.ds(r, chunk)
        mine = s[pl.ds(r + 8, chunk)]
        moved = pltpu.roll(mine, cb - 1, axis=1)
        last = jnp.where(lane_of((chunk, LANES)) == LANES - 1, natural[2, here], moved[:, cb - LANES :])
        side = cy[here] * mine * jnp.concatenate([moved[:, : cb - LANES], last], axis=1)
        by[here] = side
        moved = pltpu.roll(side, 1, axis=1)
        first = natural[0, here] * natural[1, here] * mine[:, :LANES]
        first = jnp.where(lane_of((chunk, LANES)) == 0, first, moved[:, :LANES])
        bys[here] = jnp.concatenate([first, moved[:, LANES:]], axis=1)
        bx[here] = cx[pl.ds(r + 7, chunk)] * s[pl.ds(r + 7, chunk)] * mine
    bx[rb : rb + 1] = cx[rb + 7 : rb + 8] * s[rb + 7 : rb + 8] * s[rb + 8 : rb + 9]

    def shift_loop(j, b):
        def body(i, carry):
            parts = []
            for t in range(SHIFT):
                at = b * LANES + i * SHIFT + t
                for c in range(0, cb, LANES):
                    parts.append(jnp.concatenate(
                        [basis[j][at, :RHS, c : c + LANES], basis[j][at, RHS:, c : c + LANES]], axis=1))
            out = jnp.dot(jnp.concatenate(parts, axis=0), turn[...], preferred_element_type=F32)
            n = 0
            for t in range(SHIFT):
                for c in range(0, cb, LANES):
                    for m in range(2):
                        rolled[i * SHIFT + t, m, :, c : c + LANES] = out[n : n + RHS, m * LANES : (m + 1) * LANES]
                    n += RHS
            return carry

        lax.fori_loop(0, LANES // SHIFT, body, 0)

    shift_loop(0, 0)
    def start_reduce(n, slots, turn_no, me, size, along_row):
        got = []
        for d in range(1, size):
            to = lax.rem(me + d, size)
            got.append(send(gsend.at[n], slots.at[turn_no, me], *((to, col) if along_row else (row, to))))
        slots[turn_no, me] = gsend[n]
        return got

    def finish_reduce(got, slots, turn_no, me, size):
        for copy in got:
            copy.wait_recv()
        total = slots[turn_no, 0]
        for n in range(1, size):
            total = total + slots[turn_no, n]
        return total

    for j in range(STEPS):
        if j == STEPS - 1:
            early = start_reduce(0, ga, 0, row, nrow, True)
        for copy in got_u:
            copy.wait_recv()
        for copy in got_u:
            done(copy)
        source = fields[j]
        source[0] = edge[j, 0]
        source[rb + 1] = edge[j, 1]
        final = j == STEPS - 1
        for b in range(nb):
            if b > 0:
                shift_loop(j, b)
                if final and b == 1:
                    gsend[1] = finish_reduce(early, ga, 0, row, nrow)
                    early = start_reduce(1, gb, 0, col, ncol, False)
            before = pltpu.roll(uh[j, 0, b], 1, axis=1)
            after = pltpu.roll(uh[j, 1, b], LANES - 1, axis=1)
            outside = (jnp.where(even_lane, before, after), jnp.where(even_lane, after, before))

            def apply(i, held, b=b, outside=outside, source=source, j=j, final=final):
                if not final:
                    for t in range(UNROLL):
                        r = (i - 1) * UNROLL + t
                        at = jnp.maximum(b * LANES + r, 0) + 1
                        first, last = fields[j + 1][at, :, :LANES], fields[j + 1][at, :, cb - LANES :]
                        held = pack_edges(first, last, r, t % 2, held)
                for t in range(UNROLL):
                    r = i * UNROLL + t
                    at = b * LANES + r
                    total = bx[pl.ds(at, 1), :] * source[at] + bx[pl.ds(at + 1, 1), :] * source[at + 2]
                    ends = pltpu.roll(outside[t % 2], (LANES - r) & (LANES - 1), axis=1)
                    ahead = tiles_of(rolled[r, 0]) + [ends]
                    ahead = [jnp.where(lane == LANES - 1, ahead[c + 1], ahead[c]) for c in range(len(ahead) - 1)]
                    behind = [ends] + tiles_of(rolled[r, 1])
                    behind = [jnp.where(lane == 0, behind[c], behind[c + 1]) for c in range(len(behind) - 1)]
                    total = total + by[pl.ds(at, 1), :] * jnp.concatenate(ahead, axis=1)
                    value = total + bys[pl.ds(at, 1), :] * jnp.concatenate(behind, axis=1)
                    store_split(j + 1, at, value)
                    if not final:
                        fields[j + 1][at + 1] = value
                return held

            held = lax.fori_loop(0, LANES // UNROLL, apply, empty)
            if not final:
                for t in range(UNROLL):
                    r = LANES - UNROLL + t
                    at = b * LANES + r + 1
                    first, last = fields[j + 1][at, :, :LANES], fields[j + 1][at, :, cb - LANES :]
                    held = pack_edges(first, last, r, t % 2, held)
                keep_edges(j + 1, b, held)
        if not final:
            got_u = send_edges(j + 1)
            total = gram_loop([j, lows + j, j + 1], [j + 1, lows + j + 1])
            shift_loop(j + 1, 0)
            even = total[2 * RHS :]
            keep_moment(2 * j + 2, even[:, :RHS] + 2.0 * even[:, RHS:])
        else:
            total = gram_loop([j, lows + j], [j + 1, lows + j + 1])
        keep_moment(2 * j + 1, total[:RHS, :RHS] + total[:RHS, RHS:] + total[RHS : 2 * RHS, :RHS])
    late = start_reduce(2, ga, 1, row, nrow, True)

    wide = lane_of((RHS, LANES))

    def turned(total):
        flip = jnp.transpose(total)
        flip = jnp.concatenate([flip[k * RHS : (k + 1) * RHS] for k in range(LANES // RHS)], axis=1)
        return 0.5 * (total + flip)

    moments = turned(finish_reduce(early, gb, 0, col, ncol))
    stiff = moments - pltpu.roll(moments, LANES - RHS, axis=1)
    order = STEPS * RHS
    blocks = [stiff] + [pltpu.roll(stiff, LANES - RHS * n, axis=1) for n in range(1, STEPS)] + [moments]
    stack = jnp.concatenate([jnp.where(wide < order, v, 0.0) for v in blocks], axis=0)
    stack = eliminate(stack, order - RHS, 0)
    gsend[3] = finish_reduce(late, ga, 1, row, nrow)
    late = start_reduce(3, gb, 1, col, ncol, False)
    last = turned(finish_reduce(late, gb, 1, col, ncol))
    last = jnp.where((wide >= order - RHS) & (wide < order), pltpu.roll(last, LANES - (STEPS * RHS), axis=1), 0.0)
    stack = jnp.concatenate([stack[:RHS] - last, stack[RHS:]], axis=0)
    solved = eliminate(stack, RHS, order - RHS)
    unit = jnp.where(wide == lax.broadcasted_iota(jnp.int32, (RHS, LANES), 0), 1.0, 0.0)
    remain = unit - solved + pltpu.roll(solved, RHS, axis=1)
    coef = jnp.concatenate([solved, remain], axis=0)
    high = coef.astype(BF16).astype(F32)
    low = coef - high
    lhs[...] = jnp.concatenate([high + pltpu.roll(high, LANES // 2, axis=1), low], axis=0).astype(BF16)

    for copy in sent:
        copy.wait_send()


def combine_kernel(ub0, ub1, ub2, ub3, lhs, dm, dp, x_out, r_out, x_buf, r_buf, sem):
    rb, cb = dm.shape
    block = 64
    coef = lhs[...]
    started = []
    for n in range(rb // block):
        def body(i, carry, n=n):
            rows = [n * block + i * ROWS + t for t in range(ROWS)]
            out = jnp.dot(coef, jnp.concatenate(
                [
                    jnp.concatenate([v[r, m : m + RHS, :] for m in (0, RHS) for v in (ub0, ub1, ub2, ub3)], axis=0)
                    for r in rows
                ], axis=1), preferred_element_type=F32)
            for t, r in enumerate(rows):
                part = out[:, t * cb : (t + 1) * cb]
                x_buf[r] = (part[:RHS] + part[2 * RHS : 3 * RHS]) * dm[pl.ds(r, 1), :]
                r_buf[r] = (part[RHS : 2 * RHS] + part[3 * RHS :]) * dp[pl.ds(r, 1), :]
            return carry

        lax.fori_loop(0, block // ROWS, body, 0)
        here = pl.ds(n * block, block)
        for k in range(RHS):
            for m, (buf, out) in enumerate(((x_buf, x_out), (r_buf, r_out))):
                copy = pltpu.make_async_copy(buf.at[here, k, :], out.at[k, here, :], sem.at[n, m, k])
                copy.start()
                started.append(copy)
    for copy in started:
        copy.wait()


def shards(nrow, ncol, right_side, cond_x, cond_y, pad_mask):
    rb, cb = cond_x.shape
    nb = rb // LANES
    sends = 2 + 4 + 4 * STEPS + 2 * (nrow - 1) + 2 * (ncol - 1)
    hbm = pl.BlockSpec(memory_space=pltpu.HBM)
    vmem = pl.BlockSpec(memory_space=pltpu.VMEM)
    field = pltpu.VMEM((rb + 2, RHS, cb), F32)
    *kept, = pl.pallas_call(
        functools.partial(main_kernel, (nrow, ncol)),
        out_shape=(
            *[pltpu.VMEM((rb, 2 * RHS, cb), BF16)] * (STEPS + 1), pltpu.VMEM((4 * RHS, LANES), BF16),
            pltpu.VMEM((rb, cb), F32), pltpu.VMEM((rb, cb), F32),
        ),
        in_specs=[hbm] * 4,
        out_specs=(vmem,) * (STEPS + 4),
        scratch_shapes=[
            pltpu.VMEM((8, cb), F32),
            pltpu.VMEM((rb + 8, cb), F32), pltpu.VMEM((rb, cb), F32), pltpu.VMEM((rb, cb), jnp.int32),
            pltpu.VMEM((rb + 16, cb), F32), field, field,
            pltpu.VMEM((rb + 8, cb), F32), pltpu.VMEM((rb, cb), F32), pltpu.VMEM((rb, cb), F32),
            pltpu.VMEM((3, rb, LANES), F32), pltpu.VMEM((3, 8, rb), F32),
            pltpu.VMEM((8, rb), F32), pltpu.VMEM((2, 8, rb), F32),
            pltpu.VMEM((STEPS, 2, nb, RHS, LANES), F32), pltpu.VMEM((STEPS, 2, nb, RHS, LANES), F32),
            pltpu.VMEM((STEPS, 2, RHS, cb), F32), pltpu.VMEM((LANES, 2, RHS, cb), F32), pltpu.VMEM((2 * LANES, 2 * LANES), BF16),
            pltpu.VMEM((4, RHS, LANES), F32), pltpu.VMEM((2, nrow, RHS, LANES), F32), pltpu.VMEM((2, ncol, RHS, LANES), F32),
            pltpu.SemaphoreType.DMA((3 + RHS,)), pltpu.SemaphoreType.DMA((sends,)), pltpu.SemaphoreType.DMA((sends,)),
        ],
        compiler_params=pltpu.CompilerParams(
            collective_id=0, has_side_effects=True, vmem_limit_bytes=24 * 2**20),
    )(*(pltpu.with_memory_space_constraint(v, pltpu.HBM) for v in (right_side, cond_x, cond_y, pad_mask)))
    out = jax.ShapeDtypeStruct((RHS, rb, cb), F32)
    return pl.pallas_call(
        combine_kernel,
        out_shape=(out, out),
        in_specs=[vmem] * (STEPS + 4),
        out_specs=(hbm, hbm),
        scratch_shapes=[
            pltpu.VMEM((rb, RHS, cb), F32), pltpu.VMEM((rb, RHS, cb), F32),
            pltpu.SemaphoreType.DMA((rb // 64, 2, RHS)),
        ],
        compiler_params=pltpu.CompilerParams(vmem_limit_bytes=14 * 2**20),
    )(*kept)


def solution(mesh):
    nrow, ncol = mesh.shape["row"], mesh.shape["col"]
    field, plane = P(None, "row", "col"), P("row", "col")
    return jax.shard_map(
        functools.partial(shards, nrow, ncol), mesh=mesh,
        in_specs=(field, plane, plane, plane), out_specs=(field, field), check_vma=False,
    )
```

time: 85.5 us -> 65.7 us (0.77)
  Pallas kernels: 84.8 us -> 64 us
    pallas_call x1, Pallas kernels: 76.9 us -> 56.9 us  [shards(): pl.pallas_call(functools.partial(main_kernel, (nrow, ncol)), out_shape=(*...]
where the time goes in v2:
time: 65.7 us; the launch traced here: 64.8 us
  Pallas kernels  64 us (97%)
  between operations  0.8 us (1%)
    pallas_call x1, Pallas kernels, shards(): pl.pallas_call(functools.partial(main_kernel, (nrow, ncol)), out_shape=(*...  56.9 us
    pallas_call x1, Pallas kernels, shards(): pl.pallas_call(combine_kernel, out_shape=(out, out), in_specs=[vmem] * (S...  7.11 us

profile of v2, /device:TPU:1, one launch (start us, length us, event | category | flops | bytes accessed | tf_op | source)
XLA Modules:
  0.0 64.8 jit_solution(5696909916732937813)
XLA Ops:
  0.6 56.9 %shard_map.59 = (bf16[256,32,384]{2,1,0:T(8,128)(2,1)S(1)}, bf16[256,32,384]{2,1,0:T(8,128)(2,1)S(1)}, bf16[256,32,384]{2,1,0:T(8,128)(2,1)S(1)}, bf16[256,32,38...) custom-call(f32[16,256,384]{2,1,0:T(8,128)} %rhs.1, ...), custom_call_target="tpu_custom_call" | custom-call | tf_op jit(solution)/shard_map/pallas_call | solution.py:429
  57.5 7.1 %shard_map.60 = (f32[16,256,384]{2,1,0:T(8,128)}, f32[16,256,384]{2,1,0:T(8,128)}) custom-call(bf16[256,32,384]{2,1,0:T(8,128)(2,1)S(1)} %get-tuple-element.9.ub0, bf16[256,32,384]{2,1,0:T(8,128)(2,1)S(1)} %get-tuple-element.10.ub1, bf16[256,32,384]{2,1,0:T(8,128)(2,1)S(1)} %get-tuple-element.11.ub2, bf16[256,32,384]{2,1,0:T(8,128)(2,1)S(1)} %get-tuple-element.12.ub3, ...), custom_call_target="tpu_custom_call" | custom-call | tf_op jit(solution)/shard_map/pallas_call | solution.py:453

commit v3 on v2

--- a/solution.py
+++ b/solution.py
@@ -15,7 +15,6 @@
 BF16 = jnp.bfloat16
 UNROLL = 16
 BEGIN = 16
-SHIFT = 64
 GROUP = 64
 ROWS = 64
 
@@ -41,24 +40,24 @@
     return lax.dot_general(left, right, (((1,), (1,)), ((), ())), preferred_element_type=F32)
 
 
-def eliminate(stack, order, first):
-    rows = stack.shape[0]
+def eliminate(stack, order, first, panel=8):
     lane = lane_of((1, LANES))
-    start = 0
-    for p in range(order):
-        keep = p // 8 * 8
-        if keep > start:
-            stack = stack[keep - start :]
-            start = keep
-        row = stack[p - start : p - start + 1, :]
-        at = first + p
-        col = stack[:, at : at + 1] / row[:, at : at + 1]
-        stack = jnp.where(lane == at, col, stack - col * row)
-    return stack[order - start :]
+    for start in range(0, order, panel):
+        height = stack.shape[0]
+        cols = [
+            jnp.broadcast_to(stack[:, first + start + k : first + start + k + 1], (height, LANES)) for k in range(panel)
+        ]
+        for k in range(panel):
+            scaled = cols[k] * (1.0 / cols[k][k : k + 1])
+            stack = jnp.where(lane == first + start + k, scaled, stack - scaled * stack[k : k + 1])
+            for m in range(k + 1, panel):
+                cols[m] = cols[m] - scaled * cols[m][k : k + 1]
+        stack = stack[panel:]
+    return stack
 
 
 def main_kernel(grid, rhs, cx_in, cy_in, pad_in, ub0, ub1, ub2, ub3, lhs, dm, dp, cxh,
-                cx, cy, pad, s, u0, u1, bx, by, bys, natural, pk, cyh, sh, upk, uh, edge, rolled, turn, gsend, ga, gb,
+                cx, cy, pad, s, u0, u1, bx, by, bys, natural, pk, cyh, sh, upk, uh, edge, rolled0, rolled1, turn, gsend, ga, gb, last_send, last_a, last_b,
                 in_sem, bar_send, bar_recv):
     nrow, ncol = grid
     rb, cb = dm.shape
@@ -140,7 +139,7 @@
 
     for copy in fill:
         copy.wait()
-    rolled[0, 0] = u0[1]
+    rolled0[0, 0] = u0[1]
 
     def inner(i, carry):
         for t in range(BEGIN):
@@ -191,7 +190,7 @@
 
     empty = (jnp.zeros((RHS, LANES), F32), jnp.zeros((RHS, LANES), F32))
 
-    top = rolled[0, 0] * dm[0:1, :]
+    top = rolled0[0, 0] * dm[0:1, :]
     u0[1, :, LANES:] = top[:, LANES:]
     store_split(0, 0, top[:, LANES:], LANES)
     for b in range(nb):
@@ -210,27 +209,29 @@
 
     lows = STEPS + 1
 
+    def gram_rows(left_blocks, right_blocks, rows):
+        def operand(blocks):
+            parts = [
+                jnp.concatenate(
+                    [basis[n % lows][r, n // lows * RHS : (n // lows + 1) * RHS, :] for n in blocks], axis=0)
+                for r in rows
+            ]
+            return jnp.concatenate(parts, axis=1)
+
+        return gram_dot(operand(left_blocks), operand(right_blocks))
+
     def gram_loop(left_blocks, right_blocks):
-        height = len(left_blocks) * RHS
-        width = len(right_blocks) * RHS
-
         def body(i, total):
-            rows = [i * GROUP + t for t in range(GROUP)]
-
-            def operand(blocks):
-                parts = [
-                    jnp.concatenate(
-                        [basis[n % lows][r, n // lows * RHS : (n // lows + 1) * RHS, :] for n in blocks], axis=0)
-                    for r in rows
-                ]
-                return jnp.concatenate(parts, axis=1)
-
-            return total + gram_dot(operand(left_blocks), operand(right_blocks))
-
-        return lax.fori_loop(0, rb // GROUP, body, jnp.zeros((height, width), F32))
+            return total + gram_rows(left_blocks, right_blocks, [i * GROUP + t for t in range(GROUP)])
+
+        shape = (len(left_blocks) * RHS, len(right_blocks) * RHS)
+        return lax.fori_loop(0, rb // GROUP, body, jnp.zeros(shape, F32))
 
     def keep_moment(k, value):
-        gsend[0 if k < 2 * STEPS - 1 else 2, :, k * RHS : (k + 1) * RHS] = value
+        if k < 2 * STEPS - 1:
+            gsend[0, :, k * RHS : (k + 1) * RHS] = value
+        else:
+            gsend[2, :, :RHS] = value
 
     gsend[...] = jnp.zeros_like(gsend)
     place = lax.broadcasted_iota(jnp.int32, turn.shape, 0) & (LANES - 1)
@@ -260,45 +261,41 @@
         bx[here] = cx[pl.ds(r + 7, chunk)] * s[pl.ds(r + 7, chunk)] * mine
     bx[rb : rb + 1] = cx[rb + 7 : rb + 8] * s[rb + 7 : rb + 8] * s[rb + 8 : rb + 9]
 
-    def shift_loop(j, b):
-        def body(i, carry):
-            parts = []
-            for t in range(SHIFT):
-                at = b * LANES + i * SHIFT + t
-                for c in range(0, cb, LANES):
-                    parts.append(jnp.concatenate(
-                        [basis[j][at, :RHS, c : c + LANES], basis[j][at, RHS:, c : c + LANES]], axis=1))
-            out = jnp.dot(jnp.concatenate(parts, axis=0), turn[...], preferred_element_type=F32)
-            n = 0
-            for t in range(SHIFT):
-                for c in range(0, cb, LANES):
-                    for m in range(2):
-                        rolled[i * SHIFT + t, m, :, c : c + LANES] = out[n : n + RHS, m * LANES : (m + 1) * LANES]
-                    n += RHS
-            return carry
-
-        lax.fori_loop(0, LANES // SHIFT, body, 0)
-
-    shift_loop(0, 0)
-    def start_reduce(n, slots, turn_no, me, size, along_row):
+    def shift_rows(j, start, rolled):
+        parts = []
+        for t in range(UNROLL):
+            for c in range(0, cb, LANES):
+                parts.append(jnp.concatenate(
+                    [basis[j][start + t, :RHS, c : c + LANES], basis[j][start + t, RHS:, c : c + LANES]], axis=1))
+        out = jnp.dot(jnp.concatenate(parts, axis=0), turn[...], preferred_element_type=F32)
+        n = 0
+        for t in range(UNROLL):
+            for c in range(0, cb, LANES):
+                for m in range(2):
+                    rolled[t, m, :, c : c + LANES] = out[n : n + RHS, m * LANES : (m + 1) * LANES]
+                n += RHS
+
+    shift_rows(0, 0, rolled0)
+
+    def start_reduce(part, slots, me, size, along_row):
         got = []
         for d in range(1, size):
             to = lax.rem(me + d, size)
-            got.append(send(gsend.at[n], slots.at[turn_no, me], *((to, col) if along_row else (row, to))))
-        slots[turn_no, me] = gsend[n]
+            got.append(send(part, slots.at[me], *((to, col) if along_row else (row, to))))
+        slots[me] = part[...]
         return got
 
-    def finish_reduce(got, slots, turn_no, me, size):
+    def finish_reduce(got, slots, size):
         for copy in got:
             copy.wait_recv()
-        total = slots[turn_no, 0]
-        for n in range(1, size):
-            total = total + slots[turn_no, n]
-        return total
+        parts = [slots[n] for n in range(size)]
+        while len(parts) > 1:
+            parts = [parts[n] + parts[n + 1] for n in range(0, len(parts), 2)]
+        return parts[0]
 
     for j in range(STEPS):
         if j == STEPS - 1:
-            early = start_reduce(0, ga, 0, row, nrow, True)
+            early = start_reduce(gsend.at[0], ga, row, nrow, True)
         for copy in got_u:
             copy.wait_recv()
         for copy in got_u:
@@ -307,43 +304,53 @@
         source[0] = edge[j, 0]
         source[rb + 1] = edge[j, 1]
         final = j == STEPS - 1
+        pair = jnp.zeros((2 * RHS, 2 * RHS), F32)
         for b in range(nb):
-            if b > 0:
-                shift_loop(j, b)
-                if final and b == 1:
-                    gsend[1] = finish_reduce(early, ga, 0, row, nrow)
-                    early = start_reduce(1, gb, 0, col, ncol, False)
+            if final and b == 1:
+                gsend[1] = finish_reduce(early, ga, nrow)
+                early = start_reduce(gsend.at[1], gb, col, ncol, False)
             before = pltpu.roll(uh[j, 0, b], 1, axis=1)
             after = pltpu.roll(uh[j, 1, b], LANES - 1, axis=1)
             outside = (jnp.where(even_lane, before, after), jnp.where(even_lane, after, before))
 
             def apply(i, held, b=b, outside=outside, source=source, j=j, final=final):
-                if not final:
-                    for t in range(UNROLL):
-                        r = (i - 1) * UNROLL + t
+                held = list(held)
+                base = b * LANES + i * 2 * UNROLL
+                if final:
+                    ready = jnp.maximum(base - 2 * UNROLL, 0)
+                    fresh = gram_rows([j, lows + j], [j + 1, lows + j + 1], [ready + t for t in range(2 * UNROLL)])
+                    held[0] = held[0] + jnp.where(base > 0, fresh, 0.0)
+                else:
+                    for t in range(2 * UNROLL):
+                        r = (i - 1) * 2 * UNROLL + t
                         at = jnp.maximum(b * LANES + r, 0) + 1
                         first, last = fields[j + 1][at, :, :LANES], fields[j + 1][at, :, cb - LANES :]
                         held = pack_edges(first, last, r, t % 2, held)
-                for t in range(UNROLL):
-                    r = i * UNROLL + t
-                    at = b * LANES + r
-                    total = bx[pl.ds(at, 1), :] * source[at] + bx[pl.ds(at + 1, 1), :] * source[at + 2]
-                    ends = pltpu.roll(outside[t % 2], (LANES - r) & (LANES - 1), axis=1)
-                    ahead = tiles_of(rolled[r, 0]) + [ends]
-                    ahead = [jnp.where(lane == LANES - 1, ahead[c + 1], ahead[c]) for c in range(len(ahead) - 1)]
-                    behind = [ends] + tiles_of(rolled[r, 1])
-                    behind = [jnp.where(lane == 0, behind[c], behind[c + 1]) for c in range(len(behind) - 1)]
-                    total = total + by[pl.ds(at, 1), :] * jnp.concatenate(ahead, axis=1)
-                    value = total + bys[pl.ds(at, 1), :] * jnp.concatenate(behind, axis=1)
-                    store_split(j + 1, at, value)
-                    if not final:
-                        fields[j + 1][at + 1] = value
-                return held
-
-            held = lax.fori_loop(0, LANES // UNROLL, apply, empty)
-            if not final:
-                for t in range(UNROLL):
-                    r = LANES - UNROLL + t
+                for half, (now, later) in enumerate(((rolled0, rolled1), (rolled1, rolled0))):
+                    shift_rows(j, jnp.minimum(base + (half + 1) * UNROLL, rb - UNROLL), later)
+                    for t in range(UNROLL):
+                        r = (i * 2 + half) * UNROLL + t
+                        at = b * LANES + r
+                        total = bx[pl.ds(at, 1), :] * source[at] + bx[pl.ds(at + 1, 1), :] * source[at + 2]
+                        ends = pltpu.roll(outside[t % 2], (LANES - r) & (LANES - 1), axis=1)
+                        ahead = tiles_of(now[t, 0]) + [ends]
+                        ahead = [jnp.where(lane == LANES - 1, ahead[c + 1], ahead[c]) for c in range(len(ahead) - 1)]
+                        behind = [ends] + tiles_of(now[t, 1])
+                        behind = [jnp.where(lane == 0, behind[c], behind[c + 1]) for c in range(len(behind) - 1)]
+                        total = total + by[pl.ds(at, 1), :] * jnp.concatenate(ahead, axis=1)
+                        value = total + bys[pl.ds(at, 1), :] * jnp.concatenate(behind, axis=1)
+                        store_split(j + 1, at, value)
+                        if not final:
+                            fields[j + 1][at + 1] = value
+                return tuple(held)
+
+            trips = LANES // (2 * UNROLL)
+            if final:
+                pair, = lax.fori_loop(0, trips, apply, (pair,))
+            else:
+                held = lax.fori_loop(0, trips, apply, empty)
+                for t in range(2 * UNROLL):
+                    r = LANES - 2 * UNROLL + t
                     at = b * LANES + r + 1
                     first, last = fields[j + 1][at, :, :LANES], fields[j + 1][at, :, cb - LANES :]
                     held = pack_edges(first, last, r, t % 2, held)
@@ -351,13 +358,18 @@
         if not final:
             got_u = send_edges(j + 1)
             total = gram_loop([j, lows + j, j + 1], [j + 1, lows + j + 1])
-            shift_loop(j + 1, 0)
+            shift_rows(j + 1, 0, rolled0)
             even = total[2 * RHS :]
             keep_moment(2 * j + 2, even[:, :RHS] + 2.0 * even[:, RHS:])
         else:
-            total = gram_loop([j, lows + j], [j + 1, lows + j + 1])
+            rows = [rb - 2 * UNROLL + t for t in range(2 * UNROLL)]
+            total = pair + gram_rows([j, lows + j], [j + 1, lows + j + 1], rows)
         keep_moment(2 * j + 1, total[:RHS, :RHS] + total[:RHS, RHS:] + total[RHS : 2 * RHS, :RHS])
-    late = start_reduce(2, ga, 1, row, nrow, True)
+    half = RHS // 2
+    spread = pltpu.roll(gsend[2], 0, axis=1, stride=RHS, stride_axis=0)
+    last_send[0] = jnp.concatenate(
+        [jnp.sum(spread[n : n + half], axis=0, keepdims=True) for n in (0, half)], axis=0)
+    late = start_reduce(last_send.at[0], last_a, row, nrow, True)
 
     wide = lane_of((RHS, LANES))
 
@@ -366,16 +378,23 @@
         flip = jnp.concatenate([flip[k * RHS : (k + 1) * RHS] for k in range(LANES // RHS)], axis=1)
         return 0.5 * (total + flip)
 
-    moments = turned(finish_reduce(early, gb, 0, col, ncol))
+    moments = turned(finish_reduce(early, gb, ncol))
     stiff = moments - pltpu.roll(moments, LANES - RHS, axis=1)
     order = STEPS * RHS
     blocks = [stiff] + [pltpu.roll(stiff, LANES - RHS * n, axis=1) for n in range(1, STEPS)] + [moments]
     stack = jnp.concatenate([jnp.where(wide < order, v, 0.0) for v in blocks], axis=0)
     stack = eliminate(stack, order - RHS, 0)
-    gsend[3] = finish_reduce(late, ga, 1, row, nrow)
-    late = start_reduce(3, gb, 1, col, ncol, False)
-    last = turned(finish_reduce(late, gb, 1, col, ncol))
-    last = jnp.where((wide >= order - RHS) & (wide < order), pltpu.roll(last, LANES - (STEPS * RHS), axis=1), 0.0)
+    last_send[1] = finish_reduce(late, last_a, nrow)
+    late = start_reduce(last_send.at[1], last_b, col, ncol, False)
+    last = finish_reduce(late, last_b, ncol)
+    backward = [
+        pltpu.roll(jnp.broadcast_to(last[n : n + 1], (half, LANES)), RHS, axis=1, stride=RHS, stride_axis=0)
+        for n in range(2)
+    ]
+    last = jnp.concatenate([v[half - 1 - n : half - n] for v in backward for n in range(half)], axis=0)
+    last = turned(last)
+    inside = (wide >= order - RHS) & (wide < order)
+    last = jnp.where(inside, pltpu.roll(last, order - RHS, axis=1), 0.0)
     stack = jnp.concatenate([stack[:RHS] - last, stack[RHS:]], axis=0)
     solved = eliminate(stack, RHS, order - RHS)
     unit = jnp.where(wide == lax.broadcasted_iota(jnp.int32, (RHS, LANES), 0), 1.0, 0.0)
@@ -442,8 +461,10 @@
             pltpu.VMEM((3, rb, LANES), F32), pltpu.VMEM((3, 8, rb), F32),
             pltpu.VMEM((8, rb), F32), pltpu.VMEM((2, 8, rb), F32),
             pltpu.VMEM((STEPS, 2, nb, RHS, LANES), F32), pltpu.VMEM((STEPS, 2, nb, RHS, LANES), F32),
-            pltpu.VMEM((STEPS, 2, RHS, cb), F32), pltpu.VMEM((LANES, 2, RHS, cb), F32), pltpu.VMEM((2 * LANES, 2 * LANES), BF16),
-            pltpu.VMEM((4, RHS, LANES), F32), pltpu.VMEM((2, nrow, RHS, LANES), F32), pltpu.VMEM((2, ncol, RHS, LANES), F32),
+            pltpu.VMEM((STEPS, 2, RHS, cb), F32), pltpu.VMEM((UNROLL, 2, RHS, cb), F32), pltpu.VMEM((UNROLL, 2, RHS, cb), F32),
+            pltpu.VMEM((2 * LANES, 2 * LANES), BF16),
+            pltpu.VMEM((3, RHS, LANES), F32), pltpu.VMEM((nrow, RHS, LANES), F32), pltpu.VMEM((ncol, RHS, LANES), F32),
+            pltpu.VMEM((2, 2, LANES), F32), pltpu.VMEM((nrow, 2, LANES), F32), pltpu.VMEM((ncol, 2, LANES), F32),
             pltpu.SemaphoreType.DMA((3 + RHS,)), pltpu.SemaphoreType.DMA((sends,)), pltpu.SemaphoreType.DMA((sends,)),
         ],
         compiler_params=pltpu.CompilerParams(

time: 65.7 us -> 61.8 us (0.941); the launches traced: 64.8 us -> 61.7 us
  Pallas kernels: 64 us -> 60.9 us
    pallas_call x1, Pallas kernels: 56.9 us -> 53.8 us  [shards(): pl.pallas_call(functools.partial(main_kernel, (nrow, ncol)), out_shape=(*...]
where the time goes in v3:
time: 61.8 us; the launch traced here: 61.7 us
  Pallas kernels  60.9 us (99%)
  between operations  0.8 us (1%)
    pallas_call x1, Pallas kernels, shards(): pl.pallas_call(functools.partial(main_kernel, (nrow, ncol)), out_shape=(*...  53.8 us
    pallas_call x1, Pallas kernels, shards(): pl.pallas_call(combine_kernel, out_shape=(out, out), in_specs=[vmem] * (S...  7.11 us

profile of v3, /device:TPU:1, one launch (start us, length us, event | category | flops | bytes accessed | tf_op | source)
XLA Modules:
  0.0 61.7 jit_solution(6226257272829330909)
XLA Ops:
  0.6 53.8 %shard_map.59 = (bf16[256,32,384]{2,1,0:T(8,128)(2,1)S(1)}, bf16[256,32,384]{2,1,0:T(8,128)(2,1)S(1)}, bf16[256,32,384]{2,1,0:T(8,128)(2,1)S(1)}, bf16[256,32,38...) custom-call(f32[16,256,384]{2,1,0:T(8,128)} %rhs.1, ...), custom_call_target="tpu_custom_call" | custom-call | tf_op jit(solution)/shard_map/pallas_call | solution.py:448
  54.4 7.1 %shard_map.60 = (f32[16,256,384]{2,1,0:T(8,128)}, f32[16,256,384]{2,1,0:T(8,128)}) custom-call(bf16[256,32,384]{2,1,0:T(8,128)(2,1)S(1)} %get-tuple-element.9.ub0, bf16[256,32,384]{2,1,0:T(8,128)(2,1)S(1)} %get-tuple-element.10.ub1, bf16[256,32,384]{2,1,0:T(8,128)(2,1)S(1)} %get-tuple-element.11.ub2, bf16[256,32,384]{2,1,0:T(8,128)(2,1)S(1)} %get-tuple-element.12.ub3, ...), custom_call_target="tpu_custom_call" | custom-call | tf_op jit(solution)/shard_map/pallas_call | solution.py:474

commit v4 on v3

--- a/solution.py
+++ b/solution.py
@@ -168,15 +168,24 @@
         send(pk.at[2], sh.at[0], row, right),
     ]
 
-    def send_edges(j):
+    def send_columns(j, b):
+        coming[j, b] = [
+            send(upk.at[j, 0, b], uh.at[j, 1, b], row, left),
+            send(upk.at[j, 1, b], uh.at[j, 0, b], row, right),
+        ]
+
+    def send_row(j, last):
         field = fields[j]
-        return [
-            send(field.at[rb], edge.at[j, 0], down, col),
-            send(field.at[1], edge.at[j, 1], above, col),
-            send(upk.at[j, 0], uh.at[j, 1], row, left),
-            send(upk.at[j, 1], uh.at[j, 0], row, right),
-        ]
-
+        if last:
+            coming[j, "above"] = [send(field.at[rb], edge.at[j, 0], down, col)]
+        else:
+            coming[j, "below"] = [send(field.at[1], edge.at[j, 1], above, col)]
+
+    def arrive(j, key):
+        for copy in coming[j, key]:
+            copy.wait_recv()
+
+    coming = {}
     even_lane = (lane & 1) == 0
 
     def pack_edges(first, last, r, parity, held):
@@ -205,7 +214,10 @@
             return held
 
         keep_edges(0, b, lax.fori_loop(0, LANES // BEGIN, begin, empty))
-    got_u = send_edges(0)
+        send_columns(0, b)
+        if b == 0:
+            send_row(0, False)
+    send_row(0, True)
 
     lows = STEPS + 1
 
@@ -296,19 +308,22 @@
     for j in range(STEPS):
         if j == STEPS - 1:
             early = start_reduce(gsend.at[0], ga, row, nrow, True)
-        for copy in got_u:
-            copy.wait_recv()
-        for copy in got_u:
-            done(copy)
         source = fields[j]
-        source[0] = edge[j, 0]
-        source[rb + 1] = edge[j, 1]
         final = j == STEPS - 1
+        if final:
+            arrive(j, "above")
+            source[0] = edge[j, 0]
+        else:
+            source[0] = jnp.zeros((RHS, cb), F32)
         pair = jnp.zeros((2 * RHS, 2 * RHS), F32)
         for b in range(nb):
             if final and b == 1:
                 gsend[1] = finish_reduce(early, ga, nrow)
                 early = start_reduce(gsend.at[1], gb, col, ncol, False)
+            arrive(j, b)
+            if b == nb - 1:
+                arrive(j, "below")
+                source[rb + 1] = edge[j, 1]
             before = pltpu.roll(uh[j, 0, b], 1, axis=1)
             after = pltpu.roll(uh[j, 1, b], LANES - 1, axis=1)
             outside = (jnp.where(even_lane, before, after), jnp.where(even_lane, after, before))
@@ -354,9 +369,20 @@
                     at = b * LANES + r + 1
                     first, last = fields[j + 1][at, :, :LANES], fields[j + 1][at, :, cb - LANES :]
                     held = pack_edges(first, last, r, t % 2, held)
+                if b == 0:
+                    arrive(j, "above")
+                    value = fields[j + 1][1] + bx[0:1, :] * edge[j, 0]
+                    fields[j + 1][1] = value
+                    store_split(j + 1, 0, value)
+                    held = pack_edges(value[:, :LANES], value[:, cb - LANES :], 0, 0, held)
                 keep_edges(j + 1, b, held)
+                send_columns(j + 1, b)
+                if b == 0:
+                    send_row(j + 1, False)
         if not final:
-            got_u = send_edges(j + 1)
+            send_row(j + 1, True)
+            for key in ("above", "below"):
+                done(coming[j, key][0])
             total = gram_loop([j, lows + j, j + 1], [j + 1, lows + j + 1])
             shift_rows(j + 1, 0, rolled0)
             even = total[2 * RHS :]
@@ -441,7 +467,7 @@
 def shards(nrow, ncol, right_side, cond_x, cond_y, pad_mask):
     rb, cb = cond_x.shape
     nb = rb // LANES
-    sends = 2 + 4 + 4 * STEPS + 2 * (nrow - 1) + 2 * (ncol - 1)
+    sends = 2 + 4 + (2 * nb + 2) * STEPS + 2 * (nrow - 1) + 2 * (ncol - 1)
     hbm = pl.BlockSpec(memory_space=pltpu.HBM)
     vmem = pl.BlockSpec(memory_space=pltpu.VMEM)
     field = pltpu.VMEM((rb + 2, RHS, cb), F32)

time: 61.8 us -> 59.3 us (0.960)
  Pallas kernels: 60.9 us -> 58.4 us
    pallas_call x1, Pallas kernels: 53.8 us -> 51.3 us  [shards(): pl.pallas_call(functools.partial(main_kernel, (nrow, ncol)), out_shape=(*...]
where the time goes in v4:
time: 59.3 us; the launch traced here: 59.2 us
  Pallas kernels  58.4 us (98%)
  between operations  0.8 us (1%)
    pallas_call x1, Pallas kernels, shards(): pl.pallas_call(functools.partial(main_kernel, (nrow, ncol)), out_shape=(*...  51.3 us
    pallas_call x1, Pallas kernels, shards(): pl.pallas_call(combine_kernel, out_shape=(out, out), in_specs=[vmem] * (S...  7.11 us

profile of v4, /device:TPU:1, one launch (start us, length us, event | category | flops | bytes accessed | tf_op | source)
XLA Modules:
  0.0 59.2 jit_solution(15537220873688645685)
XLA Ops:
  0.6 51.3 %shard_map.59 = (bf16[256,32,384]{2,1,0:T(8,128)(2,1)S(1)}, bf16[256,32,384]{2,1,0:T(8,128)(2,1)S(1)}, bf16[256,32,384]{2,1,0:T(8,128)(2,1)S(1)}, bf16[256,32,38...) custom-call(f32[16,256,384]{2,1,0:T(8,128)} %rhs.1, ...), custom_call_target="tpu_custom_call" | custom-call | tf_op jit(solution)/shard_map/pallas_call | solution.py:474
  51.9 7.1 %shard_map.60 = (f32[16,256,384]{2,1,0:T(8,128)}, f32[16,256,384]{2,1,0:T(8,128)}) custom-call(bf16[256,32,384]{2,1,0:T(8,128)(2,1)S(1)} %get-tuple-element.9.ub0, bf16[256,32,384]{2,1,0:T(8,128)(2,1)S(1)} %get-tuple-element.10.ub1, bf16[256,32,384]{2,1,0:T(8,128)(2,1)S(1)} %get-tuple-element.11.ub2, bf16[256,32,384]{2,1,0:T(8,128)(2,1)S(1)} %get-tuple-element.12.ub3, ...), custom_call_target="tpu_custom_call" | custom-call | tf_op jit(solution)/shard_map/pallas_call | solution.py:500
